TPU v7x, 512 devices: a whole 4x4x16 slice. The times are simulated.
512 devices in a mesh: lat: 16 (over y, z_hi), lon: 4 (over x), fold: 8 (over z_lo, core).
Axes of the slice: x: 4, y: 4, z: 16 (z_hi: 4, z_lo: 4; z = z_hi * 4 + z_lo), core: 2. Of those that a mesh axis runs over, the one named last changes fastest.
Arguments:
- field: float32 [8, 12, 640, 2560], P('fold', None, 'lat', 'lon'), may hold values from -6 to 6
- row_shift: int32 [8, 12, 640, 2560], P('fold', None, 'lat', 'lon'), may hold values from -4 to 4
- col_shift: int32 [8, 12, 640, 2560], P('fold', None, 'lat', 'lon'), may hold values from -4 to 4
- row_frac: bfloat16 [8, 12, 640, 2560], P('fold', None, 'lat', 'lon'), may hold values from 0 to 1
- col_frac: bfloat16 [8, 12, 640, 2560], P('fold', None, 'lat', 'lon'), may hold values from 0 to 1
- wave_map: int32 [64], replicated, may hold values from 0 to 1279, as said below
- legendre: float32 [64, 640, 1280], P('lon', 'lat'), may hold values from -0.25 to 0.25
- helm_coef: float32 [48], P('fold'), may hold values from 1e-06 to 0.0001
Outputs:
- spectrum: float32 [48, 4, 16, 2560], P('fold', 'lon', 'lat')
Inputs may be any that keep to these rules, and one draw needn't show every extreme that they name: `col_shift`: longitude offset of the departure cell. `wave_map`: distinct zonal wavenumbers.
All inputs are finite; a program needn't handle non-finite values.
Results may differ from a plain program's by a relative error of at most 0.0003.
Values sent between devices are 32-bit elements; how exact they have to be, the bound alone decides.
No kernel may reach another device: no remote copies, remote signals or barrier semaphores. Data moves between devices by JAX's collectives and lax.ppermute only.
A program may use at most 64 MiB of HBM per device.

v0:
```python
import math

import jax
import jax.numpy as jnp
from jax import lax
from jax.sharding import PartitionSpec as P

SHIFT_MAX = 4


def padded_2(cells, sides, width):
    for axis, dim in sides:
        count = lax.axis_size(axis)
        head = lax.slice_in_dim(cells, 0, width, axis=dim)
        tail = lax.slice_in_dim(cells, cells.shape[dim] - width, cells.shape[dim], axis=dim)
        cells = jnp.concatenate(
            [
                lax.ppermute(tail, axis, [(i, (i + 1) % count) for i in range(count)]),
                cells,
                lax.ppermute(head, axis, [((i + 1) % count, i) for i in range(count)]),
            ],
            axis=dim,
        )
    return cells


def partner(block, axis, apart):
    count = lax.axis_size(axis)
    route = []
    for low in range(count):
        high = low | 1 << apart
        if high != low and high < count:
            route += [(low, high), (high, low)]
    return lax.ppermute(block, axis, route)


def cut_along(x, dim, devices):
    dims = x.shape
    parts = x.reshape(*dims[:dim], devices, dims[dim] // devices, *dims[dim + 1 :])
    return jnp.moveaxis(parts, dim, 0)


def summed_on_arrival(x, axis, dim):
    parts = cut_along(x, dim, lax.axis_size(axis))
    arrived = lax.all_to_all(parts, axis, split_axis=0, concat_axis=0, tiled=True)
    return arrived.sum(axis=0)


def cubic_weights(fraction):
    return (
        -fraction * (fraction - 1.0) * (fraction - 2.0) / 6.0,
        (fraction + 1.0) * (fraction - 1.0) * (fraction - 2.0) / 2.0,
        -(fraction + 1.0) * fraction * (fraction - 2.0) / 2.0,
        (fraction + 1.0) * fraction * (fraction - 1.0) / 6.0,
    )


def spread_weights(shift, weights, offset):
    placed = jnp.zeros(shift.shape, jnp.float32)
    for step in range(4):
        placed = placed + jnp.where(shift + (step - 1) == offset, weights[step], 0.0)
    return placed


def interpolate_level(items, margin):
    padded, row_shift, col_shift, row_frac, col_frac = items
    rows, cols = row_shift.shape
    offsets = list(range(1 - margin, margin + 1))
    row_weights = cubic_weights(row_frac.astype(jnp.float32))
    col_weights = cubic_weights(col_frac.astype(jnp.float32))
    col_spread = [spread_weights(col_shift, col_weights, offset) for offset in offsets]
    total = jnp.zeros((rows, cols), jnp.float32)
    for row_offset in offsets:
        band_rows = padded[margin + row_offset : margin + row_offset + rows, :]
        line = jnp.zeros((rows, cols), jnp.float32)
        for place, col_offset in enumerate(offsets):
            line = (
                line
                + col_spread[place] * band_rows[:, margin + col_offset : margin + col_offset + cols]
            )
        total = total + spread_weights(row_shift, row_weights, row_offset) * line
    return total


def interpolate(padded, row_shift, col_shift, row_frac, col_frac, margin):
    return lax.map(partial_level(margin), (padded, row_shift, col_shift, row_frac, col_frac))


def partial_level(margin):

    def apply_level(items):
        return interpolate_level(items, margin)

    return apply_level


def zonal_table(waves, first_col, count_cols, lon_total):
    col_ids = first_col + lax.iota(jnp.int32, count_cols)
    phase = col_ids[:, None] * waves[None, :] % lon_total
    angle = phase.astype(jnp.float32) * (2.0 * math.pi / lon_total)
    return jnp.stack([jnp.cos(angle), -jnp.sin(angle)], axis=1) / math.sqrt(lon_total)


def spectral_rows(source, waves, first_col, lon_total):
    table = zonal_table(waves, first_col, source.shape[2], lon_total)
    return jnp.einsum("blk,kqs->sqbl", source, table, precision=lax.Precision.HIGHEST)


def local(field, row_shift, col_shift, row_frac, col_frac, wave_map, legendre, helm_coef):
    margin = SHIFT_MAX + 2
    grid = field[0]
    levels, rows, cols = grid.shape
    half = levels // 2
    lon_total = cols * lax.axis_size("lon")
    padded = padded_2(grid, (("lat", 1), ("lon", 2)), margin)
    lat_place = lax.axis_index("lat")
    band = padded[:, rows : rows + margin, :][:, ::-1, :]
    mirrored = partner(band, "fold", 0)
    pole_rows = jnp.where(lat_place == 0, jnp.zeros_like(padded[:, :margin]), padded[:, :margin])
    after_rows = jnp.where(
        lat_place == lax.axis_size("lat") - 1, mirrored, padded[:, rows + margin :]
    )
    padded = jnp.concatenate([pole_rows, padded[:, margin : rows + margin], after_rows], axis=1)
    gridded = interpolate(padded, row_shift[0], col_shift[0], row_frac[0], col_frac[0], margin)
    hemisphere = lax.axis_index("fold") % 2
    mirror_sign = (1 - 2 * hemisphere).astype(jnp.float32)
    outgoing = lax.dynamic_slice_in_dim(gridded, (1 - hemisphere) * half, half, 0)
    incoming = partner(outgoing, "fold", 0)
    kept = lax.dynamic_slice_in_dim(gridded, hemisphere * half, half, 0)
    source = jnp.concatenate([kept + incoming, mirror_sign * (kept - incoming)], axis=0)
    lon_start = lax.axis_index("lon") * cols
    waves = wave_map
    coeffs = summed_on_arrival(spectral_rows(source, waves, lon_start, lon_total), "lon", 0)
    slots_here = coeffs.shape[0]
    folded = coeffs.reshape(slots_here, 2, 2, half, rows)
    degree_count = legendre.shape[2]
    slot_base = lax.axis_index("lon") * slots_here
    degrees = lax.iota(jnp.int32, degree_count)
    waves = lax.dynamic_slice_in_dim(
        wave_map, slot_base, slots_here // lax.axis_size("lat") * lax.axis_size("lat")
    )
    product = jnp.einsum("sqelk,skn->selqn", folded, legendre, precision=lax.Precision.HIGHEST)
    parity = (waves[:, None] + degrees[None, :]) % 2 == 0
    keep = (degrees[None, :] >= waves[:, None]).astype(jnp.float32)
    picked = (
        jnp.where(parity[:, None, None, :], product[:, 0], product[:, 1]) * keep[:, None, None, :]
    )
    summed = summed_on_arrival(
        picked.reshape(
            slots_here // lax.axis_size("lat") * lax.axis_size("lat"), half, 2 * degree_count
        ),
        "lat",
        0,
    )
    degree_float = degrees.astype(jnp.float32)
    degree_pair = jnp.concatenate([degree_float, degree_float])
    damping = 1.0 + helm_coef[None, :, None] * (degree_pair * (degree_pair + 1.0))[None, None, :]
    result = summed / damping
    return jnp.transpose(result, (1, 0, 2))[:, None, :, :]


def solution(mesh):
    in_specs = (
        P("fold", None, "lat", "lon"),
        P("fold", None, "lat", "lon"),
        P("fold", None, "lat", "lon"),
        P("fold", None, "lat", "lon"),
        P("fold", None, "lat", "lon"),
        P(),
        P("lon", "lat", None),
        P("fold"),
    )
    out_specs = P("fold", "lon", "lat", None)
    return jax.shard_map(local, mesh=mesh, in_specs=in_specs, out_specs=out_specs, check_vma=False)
```

profile of v0, /device:TPU:1, one launch (start us, length us, event | category | flops | bytes accessed | tf_op | source)
XLA Modules:
  0.0 280.5 jit_solution(6543604523918076933)
XLA Ops:
  1.3 9.8 %collective-permute-start = (f32[12,6,640]{2,1,0:T(8,128)S(1)}, f32[12,6,640]{2,1,0:T(8,128)S(1)}, u32[]{:S(2)}, u32[]{:S(2)}) collective-permute-start(f32[12,6,640]{2,1,0:T(8,128)S(1)} %get-tuple-element.155), channel_id=1, source_target_pairs={{0,32},{32,64},{64,96},{96,128},{128,160},{160,192},{192,224},{224... | collective-permute-start | bytes 552968 | tf_op jit(solution)/shard_map/ppermute | solution.py:18
  11.0 8.0 %collective-permute-start.1 = (f32[12,6,640]{2,1,0:T(8,128)S(1)}, f32[12,6,640]{2,1,0:T(8,128)S(1)}, u32[]{:S(2)}, u32[]{:S(2)}) collective-permute-start(f32[12,6,640]{2,1,0:T(8,128)S(1)} %get-tuple-element.156), channel_id=1, source_target_pairs={{32,0},{64,32},{96,64},{128,96},{160,128},{192,160},{224,192},{256... | collective-permute-start | bytes 552968 | tf_op jit(solution)/shard_map/ppermute | solution.py:20
  19.1 5.4 %collective-permute-done = f32[12,6,640]{2,1,0:T(8,128)S(1)} collective-permute-done((f32[12,6,640]{2,1,0:T(8,128)S(1)}, f32[12,6,640]{2,1,0:T(8,128)S(1)}, u32[]{:S(2)}, u32[]{:S(2)}) %collective-permute-start) | collective-permute-done | bytes 184352 | tf_op jit(solution)/shard_map/ppermute | solution.py:18
  24.4 17.2 %collective-permute-done.1 = f32[12,6,640]{2,1,0:T(8,128)S(1)} collective-permute-done((f32[12,6,640]{2,1,0:T(8,128)S(1)}, f32[12,6,640]{2,1,0:T(8,128)S(1)}, u32[]{:S(2)}, u32[]{:S(2)}) %collective-permute-start.1) | collective-permute-done | bytes 184352 | tf_op jit(solution)/shard_map/ppermute | solution.py:20
  43.0 3.1 %collective-permute-start.2 = (f32[12,52,6]{2,1,0:T(8,128)S(1)}, f32[12,52,6]{2,1,0:T(8,128)S(1)}, u32[]{:S(2)}, u32[]{:S(2)}) collective-permute-start(f32[12,52,6]{2,1,0:T(8,128)S(1)} %get-tuple-element.153), channel_id=1, source_target_pairs={{0,8},{8,16},{16,24},{24,0},{1,9},{9,17},{17,25},{25,1},{2,10},{10... | collective-permute-start | bytes 44936 | tf_op jit(solution)/shard_map/ppermute | solution.py:18
  46.1 3.4 %collective-permute-start.3 = (f32[12,52,6]{2,1,0:T(8,128)S(1)}, f32[12,52,6]{2,1,0:T(8,128)S(1)}, u32[]{:S(2)}, u32[]{:S(2)}) collective-permute-start(f32[12,52,6]{2,1,0:T(8,128)S(1)} %get-tuple-element.154), channel_id=1, source_target_pairs={{8,0},{16,8},{24,16},{0,24},{9,1},{17,9},{25,17},{1,25},{10,2},{18... | collective-permute-start | bytes 44936 | tf_op jit(solution)/shard_map/ppermute | solution.py:20
  49.5 5.2 %collective-permute-done.2 = f32[12,52,6]{2,1,0:T(8,128)S(1)} collective-permute-done((f32[12,52,6]{2,1,0:T(8,128)S(1)}, f32[12,52,6]{2,1,0:T(8,128)S(1)}, u32[]{:S(2)}, u32[]{:S(2)}) %collective-permute-start.2) | collective-permute-done | bytes 15008 | tf_op jit(solution)/shard_map/ppermute | solution.py:18
  58.1 3.7 %rev.3 = f32[12,6,652]{2,1,0:T(8,128)} reverse(f32[12,6,652]{2,1,0:T(8,128)} %pad_maximum_fusion.5), dimensions={1} | reverse | bytes 375552 | tf_op jit(solution)/shard_map/rev | solution.py:117
  61.8 4.0 %collective-permute-start.4 = (f32[12,6,652]{2,1,0:T(8,128)}, f32[12,6,652]{2,1,0:T(8,128)}, u32[]{:S(2)}, u32[]{:S(2)}) collective-permute-start(f32[12,6,652]{2,1,0:T(8,128)} %rev.3), channel_id=1, source_target_pairs={{0,1},{1,0},{2,3},{3,2},{4,5},{5,4},{6,7},{7,6},{8,9},{9,8},{10,11... | collective-permute-start | bytes 563336 | tf_op jit(solution)/shard_map/ppermute | solution.py:34
  65.9 2.5 pad_maximum_fusion
  71.8 93.6 %while.13 = (s32[]{:T(128)}, f32[12,40,640]{2,1,0:T(8,128)}, s32[12,40,640]{2,1,0:T(8,128)}, bf16[12,40,640]{2,1,0:T(8,128)(2,1)}, s32[12,40,640]{2,1,0:T(8,128)...) while((s32[]{:T(128)}, f32[12,40,640]{2,1,0:T(8,128)}, ...), condition=%wide.region_1.2_spmd, body=%wide.region_0.1_spmd.sunk | while | flops 15488014 | bytes 17659776 | solution.py:86
  71.8 2.5 dynamic-slice_bitcast_fusion.13
  74.3 5.5 %fusion.211 = f32[12,40,640]{2,1,0:T(8,128)} fusion(f32[12,40,640]{2,1,0:T(8,128)} %get-tuple-element.250, s32[]{:T(128)} %get-tuple-element.249, f32[40,652]{1,0:T(8,128)S(1)} %get-tuple-element.216, f32[40,652]{1,0:T(8,128)S(1)} %get-tuple-element.217, f32[40,652]{1,0:T(8,128)S(1)} %get-tuple-element.218, f32[40,652]{1,0:T(8,128)S(1)} %get-tuple-element.219, ...), kind=kLoop, calls=%fused_computation.51.clone.1 | loop fusion | flops 15488000 | bytes 15155712 | tf_op jit(solution)/shard_map/while/body/jit(dynamic_update_index_in_dim)/dynamic_update_slice | solution.py:86
  79.7 2.5 dynamic-slice_bitcast_fusion.13
  82.2 5.5 %fusion.211 = f32[12,40,640]{2,1,0:T(8,128)} fusion(f32[12,40,640]{2,1,0:T(8,128)} %get-tuple-element.250, s32[]{:T(128)} %get-tuple-element.249, f32[40,652]{1,0:T(8,128)S(1)} %get-tuple-element.216, f32[40,652]{1,0:T(8,128)S(1)} %get-tuple-element.217, f32[40,652]{1,0:T(8,128)S(1)} %get-tuple-element.218, f32[40,652]{1,0:T(8,128)S(1)} %get-tuple-element.219, ...), kind=kLoop, calls=%fused_computation.51.clone.1 | loop fusion | flops 15488000 | bytes 15155712 | tf_op jit(solution)/shard_map/while/body/jit(dynamic_update_index_in_dim)/dynamic_update_slice | solution.py:86
  87.7 2.3 dynamic-slice_bitcast_fusion.13
  90.0 5.5 %fusion.211 = f32[12,40,640]{2,1,0:T(8,128)} fusion(f32[12,40,640]{2,1,0:T(8,128)} %get-tuple-element.250, s32[]{:T(128)} %get-tuple-element.249, f32[40,652]{1,0:T(8,128)S(1)} %get-tuple-element.216, f32[40,652]{1,0:T(8,128)S(1)} %get-tuple-element.217, f32[40,652]{1,0:T(8,128)S(1)} %get-tuple-element.218, f32[40,652]{1,0:T(8,128)S(1)} %get-tuple-element.219, ...), kind=kLoop, calls=%fused_computation.51.clone.1 | loop fusion | flops 15488000 | bytes 15155712 | tf_op jit(solution)/shard_map/while/body/jit(dynamic_update_index_in_dim)/dynamic_update_slice | solution.py:86
  95.5 2.4 dynamic-slice_bitcast_fusion.13
  97.9 5.5 %fusion.211 = f32[12,40,640]{2,1,0:T(8,128)} fusion(f32[12,40,640]{2,1,0:T(8,128)} %get-tuple-element.250, s32[]{:T(128)} %get-tuple-element.249, f32[40,652]{1,0:T(8,128)S(1)} %get-tuple-element.216, f32[40,652]{1,0:T(8,128)S(1)} %get-tuple-element.217, f32[40,652]{1,0:T(8,128)S(1)} %get-tuple-element.218, f32[40,652]{1,0:T(8,128)S(1)} %get-tuple-element.219, ...), kind=kLoop, calls=%fused_computation.51.clone.1 | loop fusion | flops 15488000 | bytes 15155712 | tf_op jit(solution)/shard_map/while/body/jit(dynamic_update_index_in_dim)/dynamic_update_slice | solution.py:86
  103.4 2.1 dynamic-slice_bitcast_fusion.13
  105.5 5.5 %fusion.211 = f32[12,40,640]{2,1,0:T(8,128)} fusion(f32[12,40,640]{2,1,0:T(8,128)} %get-tuple-element.250, s32[]{:T(128)} %get-tuple-element.249, f32[40,652]{1,0:T(8,128)S(1)} %get-tuple-element.216, f32[40,652]{1,0:T(8,128)S(1)} %get-tuple-element.217, f32[40,652]{1,0:T(8,128)S(1)} %get-tuple-element.218, f32[40,652]{1,0:T(8,128)S(1)} %get-tuple-element.219, ...), kind=kLoop, calls=%fused_computation.51.clone.1 | loop fusion | flops 15488000 | bytes 15155712 | tf_op jit(solution)/shard_map/while/body/jit(dynamic_update_index_in_dim)/dynamic_update_slice | solution.py:86
  110.9 2.1 dynamic-slice_bitcast_fusion.13
  113.0 5.5 %fusion.211 = f32[12,40,640]{2,1,0:T(8,128)} fusion(f32[12,40,640]{2,1,0:T(8,128)} %get-tuple-element.250, s32[]{:T(128)} %get-tuple-element.249, f32[40,652]{1,0:T(8,128)S(1)} %get-tuple-element.216, f32[40,652]{1,0:T(8,128)S(1)} %get-tuple-element.217, f32[40,652]{1,0:T(8,128)S(1)} %get-tuple-element.218, f32[40,652]{1,0:T(8,128)S(1)} %get-tuple-element.219, ...), kind=kLoop, calls=%fused_computation.51.clone.1 | loop fusion | flops 15488000 | bytes 15155712 | tf_op jit(solution)/shard_map/while/body/jit(dynamic_update_index_in_dim)/dynamic_update_slice | solution.py:86
  118.5 2.3 dynamic-slice_bitcast_fusion.13
  120.9 5.5 %fusion.211 = f32[12,40,640]{2,1,0:T(8,128)} fusion(f32[12,40,640]{2,1,0:T(8,128)} %get-tuple-element.250, s32[]{:T(128)} %get-tuple-element.249, f32[40,652]{1,0:T(8,128)S(1)} %get-tuple-element.216, f32[40,652]{1,0:T(8,128)S(1)} %get-tuple-element.217, f32[40,652]{1,0:T(8,128)S(1)} %get-tuple-element.218, f32[40,652]{1,0:T(8,128)S(1)} %get-tuple-element.219, ...), kind=kLoop, calls=%fused_computation.51.clone.1 | loop fusion | flops 15488000 | bytes 15155712 | tf_op jit(solution)/shard_map/while/body/jit(dynamic_update_index_in_dim)/dynamic_update_slice | solution.py:86
  126.3 2.5 dynamic-slice_bitcast_fusion.13
  128.8 5.5 %fusion.211 = f32[12,40,640]{2,1,0:T(8,128)} fusion(f32[12,40,640]{2,1,0:T(8,128)} %get-tuple-element.250, s32[]{:T(128)} %get-tuple-element.249, f32[40,652]{1,0:T(8,128)S(1)} %get-tuple-element.216, f32[40,652]{1,0:T(8,128)S(1)} %get-tuple-element.217, f32[40,652]{1,0:T(8,128)S(1)} %get-tuple-element.218, f32[40,652]{1,0:T(8,128)S(1)} %get-tuple-element.219, ...), kind=kLoop, calls=%fused_computation.51.clone.1 | loop fusion | flops 15488000 | bytes 15155712 | tf_op jit(solution)/shard_map/while/body/jit(dynamic_update_index_in_dim)/dynamic_update_slice | solution.py:86
  134.3 2.1 dynamic-slice_bitcast_fusion.13
  136.4 5.5 %fusion.211 = f32[12,40,640]{2,1,0:T(8,128)} fusion(f32[12,40,640]{2,1,0:T(8,128)} %get-tuple-element.250, s32[]{:T(128)} %get-tuple-element.249, f32[40,652]{1,0:T(8,128)S(1)} %get-tuple-element.216, f32[40,652]{1,0:T(8,128)S(1)} %get-tuple-element.217, f32[40,652]{1,0:T(8,128)S(1)} %get-tuple-element.218, f32[40,652]{1,0:T(8,128)S(1)} %get-tuple-element.219, ...), kind=kLoop, calls=%fused_computation.51.clone.1 | loop fusion | flops 15488000 | bytes 15155712 | tf_op jit(solution)/shard_map/while/body/jit(dynamic_update_index_in_dim)/dynamic_update_slice | solution.py:86
  141.8 2.5 dynamic-slice_bitcast_fusion.13
  144.3 5.5 %fusion.211 = f32[12,40,640]{2,1,0:T(8,128)} fusion(f32[12,40,640]{2,1,0:T(8,128)} %get-tuple-element.250, s32[]{:T(128)} %get-tuple-element.249, f32[40,652]{1,0:T(8,128)S(1)} %get-tuple-element.216, f32[40,652]{1,0:T(8,128)S(1)} %get-tuple-element.217, f32[40,652]{1,0:T(8,128)S(1)} %get-tuple-element.218, f32[40,652]{1,0:T(8,128)S(1)} %get-tuple-element.219, ...), kind=kLoop, calls=%fused_computation.51.clone.1 | loop fusion | flops 15488000 | bytes 15155712 | tf_op jit(solution)/shard_map/while/body/jit(dynamic_update_index_in_dim)/dynamic_update_slice | solution.py:86
  149.8 2.5 dynamic-slice_bitcast_fusion.13
  152.3 5.5 %fusion.211 = f32[12,40,640]{2,1,0:T(8,128)} fusion(f32[12,40,640]{2,1,0:T(8,128)} %get-tuple-element.250, s32[]{:T(128)} %get-tuple-element.249, f32[40,652]{1,0:T(8,128)S(1)} %get-tuple-element.216, f32[40,652]{1,0:T(8,128)S(1)} %get-tuple-element.217, f32[40,652]{1,0:T(8,128)S(1)} %get-tuple-element.218, f32[40,652]{1,0:T(8,128)S(1)} %get-tuple-element.219, ...), kind=kLoop, calls=%fused_computation.51.clone.1 | loop fusion | flops 15488000 | bytes 15155712 | tf_op jit(solution)/shard_map/while/body/jit(dynamic_update_index_in_dim)/dynamic_update_slice | solution.py:86
  157.8 2.1 dynamic-slice_bitcast_fusion.13
  159.9 5.5 %fusion.211 = f32[12,40,640]{2,1,0:T(8,128)} fusion(f32[12,40,640]{2,1,0:T(8,128)} %get-tuple-element.250, s32[]{:T(128)} %get-tuple-element.249, f32[40,652]{1,0:T(8,128)S(1)} %get-tuple-element.216, f32[40,652]{1,0:T(8,128)S(1)} %get-tuple-element.217, f32[40,652]{1,0:T(8,128)S(1)} %get-tuple-element.218, f32[40,652]{1,0:T(8,128)S(1)} %get-tuple-element.219, ...), kind=kLoop, calls=%fused_computation.51.clone.1 | loop fusion | flops 15488000 | bytes 15155712 | tf_op jit(solution)/shard_map/while/body/jit(dynamic_update_index_in_dim)/dynamic_update_slice | solution.py:86
  172.9 2.1 fusion.187
  175.0 2.2 copy.14
  177.2 2.1 copy.27
  179.4 2.5 reshape.543
  181.9 3.9 %all-to-all-start = ((f32[4,1,15360]{2,1,0:T(1,128)}), f32[4,1,15360]{2,1,0:T(1,128)S(1)}, u32[]{:S(2)}, u32[]{:S(2)}) async-start(f32[4,1,15360]{2,1,0:T(1,128)} %reshape.543), calls=%async_computation | async-start | bytes 491520 | tf_op jit(solution)/shard_map/all_to_all | solution.py:45
  187.4 4.3 %all-to-all-done = f32[4,1,15360]{2,1,0:T(1,128)S(1)} async-done(((f32[4,1,15360]{2,1,0:T(1,128)}), f32[4,1,15360]{2,1,0:T(1,128)S(1)}, u32[]{:S(2)}, u32[]{:S(2)}) %all-to-all-start) | async-done | bytes 245792 | tf_op jit(solution)/shard_map/all_to_all | solution.py:45
  194.3 2.5 reshape.544
  198.0 3.4 %fusion.181 = f32[16,2,6,2,1280]{4,2,1,3,0:T(8,128)S(1)} fusion(f32[16,40,1280]{2,1,0:T(8,128)S(1)} %copy-done, f32[16,2,2,6,40]{4,0,3,2,1:T(8,128)S(1)} %bitcast.474), kind=kOutput, calls=%fused_computation.397 | convolution fusion | flops 235929600 | bytes 5304320 | tf_op jit(solution)/shard_map/sqelk,skn->selqn/dot_general | solution.py:142
  204.2 2.9 %squeeze.50 = f32[16,1,6,2560]{3,0,2,1:T(8,128)} reshape(f32[16,1,6,2,1280]{4,3,0,2,1:T(2,128)} %copy.17) | data formatting | bytes 1966080 | tf_op jit(solution)/shard_map/squeeze | solution.py:146
  207.1 2.8 copy.18
  209.9 3.0 %squeeze.51 = f32[16,1,6,2560]{3,0,2,1:T(8,128)} reshape(f32[16,1,6,2,1280]{4,3,0,2,1:T(2,128)} %copy.18) | data formatting | bytes 1966080 | tf_op jit(solution)/shard_map/squeeze | solution.py:146
  216.5 11.2 %all-to-all-start.1 = ((f32[16,1,6,2560]{3,1,2,0:T(1,128)}), f32[16,1,6,2560]{3,1,2,0:T(1,128)}, u32[]{:S(2)}, u32[]{:S(2)}) async-start(f32[16,1,6,2560]{3,1,2,0:T(1,128)} %copy.19), calls=%async_computation.1 | async-start | bytes 1966080 | tf_op jit(solution)/shard_map/all_to_all | solution.py:45
  227.7 50.2 %all-to-all-done.1 = f32[16,1,6,2560]{3,1,2,0:T(1,128)} async-done(((f32[16,1,6,2560]{3,1,2,0:T(1,128)}), f32[16,1,6,2560]{3,1,2,0:T(1,128)}, u32[]{:S(2)}, u32[]{:S(2)}) %all-to-all-start.1) | async-done | bytes 983072 | tf_op jit(solution)/shard_map/all_to_all | solution.py:45
  (58 shorter events, 31.0 us)
Async XLA Ops:
  0.0 198.0 %copy-start = (f32[16,40,1280]{2,1,0:T(8,128)S(1)}, f32[16,40,1280]{2,1,0:T(8,128)}, u32[]{:S(2)}) copy-start(f32[16,40,1280]{2,1,0:T(8,128)} %param.16) | copy-start | bytes 9830404
  1.3 55.8 %copy-start.1 = (f32[1,12,40,640]{3,2,1,0:T(8,128)S(1)}, f32[1,12,40,640]{3,2,1,0:T(8,128)}, u32[]{:S(2)}) copy-start(f32[1,12,40,640]{3,2,1,0:T(8,128)} %param.10) | copy-start | bytes 3686404
  1.3 23.2 %collective-permute-start = (f32[12,6,640]{2,1,0:T(8,128)S(1)}, f32[12,6,640]{2,1,0:T(8,128)S(1)}, u32[]{:S(2)}, u32[]{:S(2)}) collective-permute-start(f32[12,6,640]{2,1,0:T(8,128)S(1)} %get-tuple-element.155), channel_id=1, source_target_pairs={{0,32},{32,64},{64,96},{96,128},{128,160},{160,192},{192,224},{224... | collective-permute-start | bytes 552968 | tf_op jit(solution)/shard_map/ppermute | solution.py:18
  11.0 30.6 %collective-permute-start.1 = (f32[12,6,640]{2,1,0:T(8,128)S(1)}, f32[12,6,640]{2,1,0:T(8,128)S(1)}, u32[]{:S(2)}, u32[]{:S(2)}) collective-permute-start(f32[12,6,640]{2,1,0:T(8,128)S(1)} %get-tuple-element.156), channel_id=1, source_target_pairs={{32,0},{64,32},{96,64},{128,96},{160,128},{192,160},{224,192},{256... | collective-permute-start | bytes 552968 | tf_op jit(solution)/shard_map/ppermute | solution.py:20
  41.7 14.7 %copy-start.3 = (f32[12,6,640]{2,1,0:T(8,128)}, f32[12,6,640]{2,1,0:T(8,128)S(1)}, u32[]{:S(2)}) copy-start(f32[12,6,640]{2,1,0:T(8,128)S(1)} %collective-permute-done.1) | copy-start | bytes 552964
  43.0 11.7 %collective-permute-start.2 = (f32[12,52,6]{2,1,0:T(8,128)S(1)}, f32[12,52,6]{2,1,0:T(8,128)S(1)}, u32[]{:S(2)}, u32[]{:S(2)}) collective-permute-start(f32[12,52,6]{2,1,0:T(8,128)S(1)} %get-tuple-element.153), channel_id=1, source_target_pairs={{0,8},{8,16},{16,24},{24,0},{1,9},{9,17},{17,25},{25,1},{2,10},{10... | collective-permute-start | bytes 44936 | tf_op jit(solution)/shard_map/ppermute | solution.py:18
  46.1 10.2 %collective-permute-start.3 = (f32[12,52,6]{2,1,0:T(8,128)S(1)}, f32[12,52,6]{2,1,0:T(8,128)S(1)}, u32[]{:S(2)}, u32[]{:S(2)}) collective-permute-start(f32[12,52,6]{2,1,0:T(8,128)S(1)} %get-tuple-element.154), channel_id=1, source_target_pairs={{8,0},{16,8},{24,16},{0,24},{9,1},{17,9},{25,17},{1,25},{10,2},{18... | collective-permute-start | bytes 44936 | tf_op jit(solution)/shard_map/ppermute | solution.py:20
  54.7 1.6 copy-start.5
  56.4 0.7 copy-start.7
  61.8 6.8 %collective-permute-start.4 = (f32[12,6,652]{2,1,0:T(8,128)}, f32[12,6,652]{2,1,0:T(8,128)}, u32[]{:S(2)}, u32[]{:S(2)}) collective-permute-start(f32[12,6,652]{2,1,0:T(8,128)} %rev.3), channel_id=1, source_target_pairs={{0,1},{1,0},{2,3},{3,2},{4,5},{5,4},{6,7},{7,6},{8,9},{9,8},{10,11... | collective-permute-start | bytes 563336 | tf_op jit(solution)/shard_map/ppermute | solution.py:34
  68.4 1.3 copy-start.2
  68.4 1.3 copy-start.4
  68.4 1.4 copy-start.6
  68.5 1.5 copy-start.8
  71.7 97.5 %copy-start.11 = (s32[64]{0:T(128)S(1)}, s32[64]{0:T(128)}, u32[]{:S(2)}) copy-start(s32[64]{0:T(128)} %param.15) | copy-start | bytes 772
  167.3 4.3 %collective-permute-start.5 = (f32[6,40,640]{2,1,0:T(8,128)}, f32[6,40,640]{2,1,0:T(8,128)}, u32[]{:S(2)}, u32[]{:S(2)}) collective-permute-start(f32[6,40,640]{2,1,0:T(8,128)} %constant_dynamic-slice_fusion), channel_id=1, source_target_pairs={{0,1},{1,0},{2,3},{3,2},{4,5},{5,4},{6,7},{7,6},{8,9},{9,8},{10,11... | collective-permute-start | bytes 1843208 | tf_op jit(solution)/shard_map/ppermute | solution.py:34
  181.9 9.8 %all-to-all-start = ((f32[4,1,15360]{2,1,0:T(1,128)}), f32[4,1,15360]{2,1,0:T(1,128)S(1)}, u32[]{:S(2)}, u32[]{:S(2)}) async-start(f32[4,1,15360]{2,1,0:T(1,128)} %reshape.543), calls=%async_computation | async-start | bytes 491520 | tf_op jit(solution)/shard_map/all_to_all | solution.py:45
  209.9 3.0 %copy-start.9 = (f32[2,8,2,1280]{3,1,2,0:T(8,128)S(1)}, f32[2,8,2,1280]{3,1,2,0:T(8,128)}, u32[]{:S(2)}) copy-start(f32[2,8,2,1280]{3,1,2,0:T(8,128)} %copy.23) | copy-start | bytes 491524
  209.9 3.0 %copy-start.10 = (pred[2,8,2,1280]{3,1,2,0:T(8,128)(4,1)S(1)}, pred[2,8,2,1280]{3,1,2,0:T(8,128)(4,1)}, u32[]{:S(2)}) copy-start(pred[2,8,2,1280]{3,1,2,0:T(8,128)(4,1)} %copy.22) | copy-start | bytes 122884
  216.5 63.3 %copy-start.12 = (f32[6]{0:T(128)S(1)}, f32[6]{0:T(128)}, u32[]{:S(2)}) copy-start(f32[6]{0:T(128)} %param.17) | copy-start | bytes 76
  216.5 61.4 %all-to-all-start.1 = ((f32[16,1,6,2560]{3,1,2,0:T(1,128)}), f32[16,1,6,2560]{3,1,2,0:T(1,128)}, u32[]{:S(2)}, u32[]{:S(2)}) async-start(f32[16,1,6,2560]{3,1,2,0:T(1,128)} %copy.19), calls=%async_computation.1 | async-start | bytes 1966080 | tf_op jit(solution)/shard_map/all_to_all | solution.py:45
where the time goes:
time: 283 us; the launch traced here: 281 us
  waiting for transfers between devices  85.4 us (30%)
  other arithmetic  81.8 us (29%)
  local copies, waits for them, and re-layouts  62 us (22%)
  starting transfers between devices  45.4 us (16%)
  matrix products  5.52 us (2%)
    dynamic_update_slice x12, other arithmetic, interpolate(): lax.map(partial_level(margin), (padded, row_shift, col_shift, row_frac, c...  65.6 us
    all_to_all x2, waiting for transfers between devices, summed_on_arrival(): lax.all_to_all(parts, axis, split_axis=0, concat_axis=0, tiled=True)  54.5 us
    slice x12, local copies, waits for them, and re-layouts, interpolate_level(): band_rows = padded[margin + row_offset:margin + row_offset + rows, :]  27.9 us
    ppermute x2, waiting for transfers between devices, padded_2(): lax.ppermute(head, axis, [((i + 1) % count, i) for i in range(count)])  18.9 us
    all_to_all x2, starting transfers between devices, summed_on_arrival(): lax.all_to_all(parts, axis, split_axis=0, concat_axis=0, tiled=True)  15.2 us
    ppermute x2, starting transfers between devices, padded_2(): lax.ppermute(tail, axis, [(i, (i + 1) % count) for i in range(count)])  12.9 us
    ppermute x2, starting transfers between devices, padded_2(): lax.ppermute(head, axis, [((i + 1) % count, i) for i in range(count)])  11.4 us
    ppermute x2, waiting for transfers between devices, padded_2(): lax.ppermute(tail, axis, [(i, (i + 1) % count) for i in range(count)])  10.6 us
  transfers between devices with their start and end apart: 8, of which 7 were waited for; matrix products, arithmetic and copies ran while one was open for 2% of the time, Pallas kernels for 0%

commit v1 on v0

v1 whole, which is shorter than its diff:
```python
import math

import jax
import jax.numpy as jnp
from jax import lax
from jax.experimental import pallas as pl
from jax.experimental.pallas import tpu as pltpu
from jax.sharding import Mesh, PartitionSpec as P

LEVELS = 12
HALF = 6
ROWS = 40
COLS = 640
TILES = 5
DEG = 1280
LON_TOTAL = 2560
WIN = 107
NWIN = 6
KDIM = NWIN * 128
VM = pltpu.CompilerParams(vmem_limit_bytes=48 * 1024 * 1024)
LAT = ("y", "zh")
LATF = ("y", "zh", "zl", "core")


def lane_iota():
    return lax.broadcasted_iota(jnp.int32, (8, 128), 1)


def roll(x, shift):
    shift %= 128
    return pltpu.roll(x, shift, 1) if shift else x


def vmem():
    return pl.BlockSpec(memory_space=pltpu.VMEM)


def smem():
    return pl.BlockSpec(memory_space=pltpu.SMEM)


def f32(*dims):
    return jax.ShapeDtypeStruct(dims, jnp.float32)


def lat_index():
    return lax.axis_index("y") * 4 + lax.axis_index("zh")


def edges_kernel(field, lat_even, lat_odd, lon_even, lon_odd):
    lat = lat_index()
    odd = lat % 2
    for j in range(6):
        at_even = jnp.where(odd == 0, 34 + j, j)
        at_odd = jnp.where(odd == 0, j, jnp.where(lat == 15, 39 - j, 34 + j))
        for l in range(LEVELS):
            lat_even[pl.ds(6 * l + j, 1), :] = field[0, l, pl.ds(at_even, 1), :]
            lat_odd[pl.ds(6 * l + j, 1), :] = field[0, l, pl.ds(at_odd, 1), :]
    lane = lane_iota()
    lon_par = lax.axis_index("lon") % 2
    for rt in range(TILES):
        rows = slice(8 * rt, 8 * rt + 8)
        left = jnp.zeros((8, 128), jnp.float32)
        right = jnp.zeros((8, 128), jnp.float32)
        for l in range(LEVELS):
            here = (lane >= 8 * l) & (lane < 8 * l + 6)
            left = jnp.where(here, roll(field[0, l, rows, 0:128], 8 * l), left)
            right = jnp.where(here, roll(field[0, l, rows, 512:640], 8 * l - 122), right)
        lon_even[rows, :] = jnp.where(lon_par == 0, right, left)
        lon_odd[rows, :] = jnp.where(lon_par == 0, left, right)


def corner_kernel(lon_even, lon_odd, to_even, to_odd):
    lat = lat_index()
    odd = lat % 2
    for r in range(8):
        at_even = jnp.where(odd == 0, 32 + r, r)
        at_odd = jnp.where(odd == 0, r, jnp.where(lat == 15, 39 - r, 32 + r))
        for k, ref in enumerate((lon_even, lon_odd)):
            to_even[pl.ds(8 * k + r, 1), :] = ref[pl.ds(at_even, 1), :]
            to_odd[pl.ds(8 * k + r, 1), :] = ref[pl.ds(at_odd, 1), :]


def cubic(t):
    down = t - 1.0
    two = t - 2.0
    up = t + 1.0
    inner = t * down
    outer = up * two
    return (
        inner * two * (-1.0 / 6.0),
        outer * down * 0.5,
        outer * t * (-0.5),
        up * inner * (1.0 / 6.0),
    )


def window(tiles, start, lane):
    first, off = divmod(start, 128)
    x = tiles[first]
    if off:
        if first + 1 < len(tiles):
            x = jnp.where(lane >= off, x, tiles[first + 1])
        x = roll(x, -off)
    return x


def take(x, index):
    return jnp.take_along_axis(x, index, axis=1, mode="promise_in_bounds")


def put_windows(win, row, tiles, lane):
    for w in range(NWIN):
        win[w, row : row + 8, :] = window(tiles, WIN * w + 123, lane)


def lon_sides(lon_even, lon_odd, rows, lon_par):
    even = lon_even[rows, :]
    odd = lon_odd[rows, :]
    return jnp.where(lon_par == 0, odd, even), jnp.where(lon_par == 0, even, odd)


def dyn_roll(x, shift):
    return pltpu.roll(x, shift, 1)


def tile_points(win, at, w, shift_row, shift_col, frac_row, frac_col, lane):
    def cut(ref_tiles):
        return window(ref_tiles, WIN * w, lane)

    rs = cut(shift_row)
    cs = cut(shift_col)
    wr = cubic(cut(frac_row))
    wc = cubic(cut(frac_col))
    first = jnp.minimum(cs + (lane + 4), 124)
    index = [first, first + 1, first + 2, first + 3]
    line = []
    for k in range(12):
        src = win[w, at + k - 5 : at + k + 3, :]
        acc = wc[0] * take(src, index[0])
        for b in range(1, 4):
            acc = acc + wc[b] * take(src, index[b])
        line.append(acc)
    u = rs + 4
    m = u >= 5
    line = [jnp.where(m, line[k + 5], line[k]) for k in range(7)] + [line[7]]
    u = jnp.where(m, u - 5, u)
    m = u >= 3
    line = [jnp.where(m, line[k + 3], line[k]) for k in range(5)] + [line[5]]
    u = jnp.where(m, u - 3, u)
    m = u >= 2
    line = [jnp.where(m, line[k + 2], line[k]) for k in range(4)] + [line[4]]
    m = u == 1
    line = [jnp.where(m, line[k + 1], line[k]) for k in range(4)]
    total = wr[0] * line[0]
    for a in range(1, 4):
        total = total + wr[a] * line[a]
    return total


def lane_tiles(ref, l, rt):
    x = ref[0, l, pl.ds(8 * rt, 8), :]
    if x.dtype == jnp.bfloat16:
        x = x.astype(jnp.float32)
    return [x[:, 128 * t : 128 * t + 128] for t in range(TILES)]


def main_rows(win, field, lon_even, lon_odd, l, row_tiles, lon_par, lane):
    for rt in row_tiles:
        left, right = lon_sides(lon_even, lon_odd, slice(8 * rt, 8 * rt + 8), lon_par)
        tiles = [dyn_roll(left, (250 - 8 * l) % 128)] + lane_tiles(field, l, rt) + [dyn_roll(right, (128 - 8 * l) % 128)]
        put_windows(win, 8 + 8 * rt, tiles, lane)


def split(x):
    hi = x.astype(jnp.bfloat16)
    return hi, (x - hi.astype(jnp.float32)).astype(jnp.bfloat16)


def dot(a, b):
    return jnp.dot(a, b, preferred_element_type=jnp.float32)


def zonal(grid, table):
    hi, lo = split(grid)
    t_hi, t_lo = split(table)
    return dot(hi, t_hi) + (dot(lo, t_hi) + dot(hi, t_lo))


def points_of(l, rt, win, row_shift, col_shift, row_frac, col_frac, lane, put):
    params = [lane_tiles(r, l, rt) for r in (row_shift, col_shift, row_frac, col_frac)]
    for w in range(NWIN):
        put(w, tile_points(win, 8 + 8 * rt, w, *params, lane))


def inner_kernel(field, row_shift, col_shift, row_frac, col_frac, lon_even, lon_odd, table, out, win, grid):
    lane = lane_iota()
    lon_par = lax.axis_index("lon") % 2

    def level(l, carry):
        main_rows(win, field, lon_even, lon_odd, l, range(TILES), lon_par, lane)
        for i in range(3):

            def put(w, x, i=i):
                grid[pl.ds(24 * l + 8 * i, 8), 128 * w : 128 * w + 128] = x

            points_of(l, i + 1, win, row_shift, col_shift, row_frac, col_frac, lane, put)
        return carry

    lax.fori_loop(0, LEVELS, level, 0)
    out[...] = zonal(grid[...], table[...])


def transposed_groups(block, lane):
    group = lane // 8
    for k in (8, 4, 2, 1):
        bit = (group & k) != 0
        new = list(block)
        for i in range(16):
            if not i & k:
                a, b = block[i], block[i + k]
                new[i] = jnp.where(bit, roll(b, 8 * k), a)
                new[i + k] = jnp.where(bit, b, roll(a, -8 * k))
        block = new
    return block


def outer_kernel(
    field,
    row_shift,
    col_shift,
    row_frac,
    col_frac,
    lon_even,
    lon_odd,
    lat_even,
    lat_odd,
    corner_even,
    corner_odd,
    table,
    inner,
    out,
    win,
    grid,
    zon,
    halo,
    side,
):
    lane = lane_iota()
    lon_par = lax.axis_index("lon") % 2
    lat_odd_place = lat_index() % 2

    def place(before, after, corner_before, corner_after):
        for l in range(LEVELS):
            halo[0, l, 2:8, :] = before[6 * l : 6 * l + 6, :]
            halo[1, l, 0:6, :] = after[6 * l : 6 * l + 6, :]
        side[0] = corner_before[...]
        side[1] = corner_after[...]

    for l in range(LEVELS):
        halo[0, l, 0:2, :] = jnp.zeros((2, COLS), jnp.float32)
        halo[1, l, 6:8, :] = jnp.zeros((2, COLS), jnp.float32)

    @pl.when(lat_odd_place == 0)
    def _():
        place(lat_odd, lat_even, corner_odd, corner_even)

    @pl.when(lat_odd_place == 1)
    def _():
        place(lat_even, lat_odd, corner_even, corner_odd)

    def level(l, carry):
        main_rows(win, field, lon_even, lon_odd, l, (0, 1, 3, 4), lon_par, lane)
        for k, row in ((0, 0), (1, 48)):
            even = side[k, 0:8, :]
            odd = side[k, 8:16, :]
            left = jnp.where(lon_par == 0, odd, even)
            right = jnp.where(lon_par == 0, even, odd)
            x = halo[k, l]
            tiles = [x[:, 128 * t : 128 * t + 128] for t in range(TILES)]
            tiles = [dyn_roll(left, (250 - 8 * l) % 128)] + tiles + [dyn_roll(right, (128 - 8 * l) % 128)]
            put_windows(win, row, tiles, lane)
        for i, rt in enumerate((0, 4)):

            def put(w, x, i=i):
                grid[pl.ds(16 * l + 8 * i, 8), 128 * w : 128 * w + 128] = x

            points_of(l, rt, win, row_shift, col_shift, row_frac, col_frac, lane, put)
        return carry

    lax.fori_loop(0, LEVELS, level, 0)
    zon[...] = zonal(grid[...], table[...])
    for core in range(2):
        for v in range(2):
            block = []
            for p in range(16 * v, 16 * v + 16):
                rt, l = divmod(min(p, 29), HALF)
                l += HALF * core
                if rt in (0, 4):
                    at = 16 * l + (8 if rt else 0)
                    block.append(zon[at : at + 8, :])
                else:
                    at = 24 * l + 8 * (rt - 1)
                    block.append(inner[at : at + 8, :])
            block = transposed_groups(block, lane)
            for d in range(16):
                lon, y = divmod(d, 4)
                out[y * 8 + lon * 2 + core, 8 * v : 8 * v + 8, :] = block[d]


def legendre_kernel(wave_map, arrived, legendre, from_1, from_2, from_3, out, lhs):
    lane = lane_iota()
    place = lax.axis_index("y")
    pieces = []
    for v in range(2):
        half = {}
        for y in range(4):
            sums = []
            for core in range(2):
                x = arrived[(place ^ y) * 8 + core, 8 * v : 8 * v + 8, :]
                for lon in range(1, 4):
                    x = x + arrived[(place ^ y) * 8 + lon * 2 + core, 8 * v : 8 * v + 8, :]
                sums.append(x)
            half[0, y] = sums[0] + sums[1]
            half[1, y] = sums[0] - sums[1]
        pieces += [half[e, y] for e in range(2) for y in range(4)]
    turned = jnp.concatenate(pieces, axis=0).T
    lhs[...] = jnp.zeros(lhs.shape, jnp.float32)
    for e in range(2):
        for l in range(HALF):
            first = jnp.zeros((8, 128), jnp.float32)
            last = jnp.zeros((8, 128), jnp.float32)
            for rt in range(TILES):
                v, p = divmod(rt * HALF + l, 16)
                x = turned[8 * p : 8 * p + 8, :]
                x = roll(x, 32 * (rt % 4) - (64 * v + 32 * e))
                here = (lane >= 32 * (rt % 4)) & (lane < 32 * (rt % 4) + 32)
                if rt < 4:
                    first = jnp.where(here, x, first)
                else:
                    last = jnp.where(here, x, last)
            for s in range(4):
                lhs[s, 16 * e + 2 * l : 16 * e + 2 * l + 2, 0:128] = first[2 * s : 2 * s + 2, :]
                lhs[s, 16 * e + 2 * l : 16 * e + 2 * l + 2, 128:256] = last[2 * s : 2 * s + 2, :]
    slot = lax.axis_index("lon") * 16 + lax.axis_index("y") * 4
    degree = lax.broadcasted_iota(jnp.int32, (16, DEG), 1)
    low = lax.broadcasted_iota(jnp.int32, (8, 128), 0) < 4
    for s in range(4):
        wave = wave_map[slot + s]
        a_hi, a_lo = split(lhs[s][:, 0:160])
        rows = []
        for rt in range(TILES):
            at = slice(40 * s + 8 * rt, 40 * s + 8 * rt + 8)
            rows += [legendre[place, at, :], from_1[at, :], from_2[at, :], from_3[at, :]]
        b_hi, b_lo = split(jnp.concatenate(rows, axis=0))
        sums = dot(a_hi, b_hi) + (dot(a_lo, b_hi) + dot(a_hi, b_lo))
        picked = jnp.where((degree + wave) % 2 == 0, sums[0:16], sums[16:32])
        picked = jnp.where(degree >= wave, picked, 0.0)
        for j in range(10):
            out[s, 8 * j : 8 * j + 8, :] = picked[0:8, 128 * j : 128 * j + 128]
        for j in range(0, 10, 2):
            a = picked[8:16, 128 * j : 128 * j + 128]
            b = picked[8:16, 128 * j + 128 : 128 * j + 256]
            out[s, 80 + 4 * j : 88 + 4 * j, :] = jnp.where(low, a, pltpu.roll(b, 4, 0))


def finish_kernel(helm, parts, out):
    total = parts[0] + parts[1] + (parts[2] + parts[3])
    row = lax.broadcasted_iota(jnp.int32, (8, 128), 0)
    lane = lane_iota()

    def damped(x, first, degree):
        coef = jnp.zeros((8, 128), jnp.float32)
        for i in range(4):
            coef = jnp.where(row // 2 == i, helm[(first + i) % HALF if first + i < HALF else 4 + i % 2], coef)
        return x / (1.0 + coef * (degree * (degree + 1.0)))

    for j in range(10):
        degree = (lane + 128 * j).astype(jnp.float32)
        x = damped(total[8 * j : 8 * j + 8, :], 0, degree)
        for i in range(8):
            l, q = divmod(i, 2)
            out[l, 0, 0, q * DEG + 128 * j : q * DEG + 128 * j + 128] = x[i, :]
    for j in range(0, 10, 2):
        degree = (lane + 128 * j + jnp.where(row < 4, 0, 128)).astype(jnp.float32)
        x = damped(total[80 + 4 * j : 88 + 4 * j, :], 4, degree)
        for i in range(8):
            l, q = divmod(i % 4, 2)
            at = q * DEG + 128 * (j + i // 4)
            out[4 + l, 0, 0, at : at + 128] = x[i, :]


def zonal_table(wave_map):
    k = lax.broadcasted_iota(jnp.int32, (KDIM, 128), 0)
    lane = lax.broadcasted_iota(jnp.int32, (KDIM, 128), 1)
    i = k % 128
    col = k // 128 * WIN + i
    valid = (i < WIN) & (col < COLS)
    phase = (col + lax.axis_index("lon") * COLS) * jnp.repeat(wave_map, 2)[None, :] % LON_TOTAL
    phase = (phase + (lane % 2) * (LON_TOTAL // 4)) % LON_TOTAL
    angle = phase.astype(jnp.float32) * (2.0 * math.pi / LON_TOTAL)
    return jnp.where(valid, jnp.cos(angle) / math.sqrt(LON_TOTAL), 0.0)


def lon_pairs(odd):
    return [r for i in range(odd, 4, 2) for r in ((i, (i + 1) % 4), ((i + 1) % 4, i))]


def lat_pairs(odd):
    route = []
    for i in range(odd, 15, 2):
        for f in range(8):
            low, high = i * 8 + f, (i + 1) * 8 + f
            route += [(low, high), (high, low)]
    if odd:
        for f in range(8):
            route.append((15 * 8 + f, 15 * 8 + (f ^ 1)))
    return route


def call(kernel, outs, count, scratch=(), smem_first=0):
    specs = [smem()] * smem_first + [vmem()] * (count - smem_first)
    return pl.pallas_call(
        kernel,
        out_shape=outs,
        in_specs=specs,
        out_specs=jax.tree.map(lambda _: vmem(), outs),
        scratch_shapes=list(scratch),
        compiler_params=VM,
    )


def stages(field, row_shift, col_shift, row_frac, col_frac, wave_map, legendre, helm_coef):
    grid_args = (field, row_shift, col_shift, row_frac, col_frac)
    lat_e, lat_o, lon_e, lon_o = call(edges_kernel, (f32(72, COLS), f32(72, COLS), f32(ROWS, 128), f32(ROWS, 128)), 1)(field)
    lat_e = lax.ppermute(lat_e, LATF, lat_pairs(0))
    lat_o = lax.ppermute(lat_o, LATF, lat_pairs(1))
    lon_e = lax.ppermute(lon_e, "lon", lon_pairs(0))
    lon_o = lax.ppermute(lon_o, "lon", lon_pairs(1))
    cor_e, cor_o = call(corner_kernel, (f32(16, 128), f32(16, 128)), 2)(lon_e, lon_o)
    cor_e = lax.ppermute(cor_e, LATF, lat_pairs(0))
    cor_o = lax.ppermute(cor_o, LATF, lat_pairs(1))
    legendre = legendre.reshape(4, 4 * ROWS, DEG)
    place = lax.axis_index("y")
    arrived_rows = [
        lax.ppermute(lax.dynamic_index_in_dim(legendre, place ^ d, 0, keepdims=False), "y", [(i, i ^ d) for i in range(4)])
        for d in (1, 2, 3)
    ]
    table = zonal_table(wave_map)
    win = pltpu.VMEM((NWIN, 56, 128), jnp.float32)
    inner = call(inner_kernel, f32(LEVELS * 24, 128), 8, (win, pltpu.VMEM((LEVELS * 24, KDIM), jnp.float32)))(
        *grid_args, lon_e, lon_o, table
    )
    sent = call(
        outer_kernel,
        f32(32, 16, 128),
        13,
        (
            win,
            pltpu.VMEM((LEVELS * 16, KDIM), jnp.float32),
            pltpu.VMEM((LEVELS * 16, 128), jnp.float32),
            pltpu.VMEM((2, LEVELS, 8, COLS), jnp.float32),
            pltpu.VMEM((2, 16, 128), jnp.float32),
        ),
    )(*grid_args, lon_e, lon_o, lat_e, lat_o, cor_e, cor_o, table, inner)
    arrived = lax.all_to_all(sent, ("y", "lon", "core"), 0, 0, tiled=True)
    parts = call(legendre_kernel, f32(4, 120, 128), 6, (pltpu.VMEM((4, 32, 256), jnp.float32),), 1)(
        wave_map, arrived, legendre, *arrived_rows
    )
    parts = lax.all_to_all(parts, "zh", 0, 0, tiled=True)
    return call(finish_kernel, f32(HALF, 1, 1, 2 * DEG), 2, (), 1)(helm_coef, parts)


def solution(mesh):
    fine = Mesh(mesh.devices.reshape(4, 4, 4, 4, 2), ("y", "zh", "lon", "zl", "core"))
    fold = ("zl", "core")
    block = P(fold, None, LAT, "lon")
    in_specs = (block, block, block, block, block, P(), P("lon", LAT, None), P(fold))
    return jax.shard_map(stages, mesh=fine, in_specs=in_specs, out_specs=P(fold, "lon", LAT, None), check_vma=False)
```

time: 283 us -> 169 us (0.60)
  the two profiles are of different devices: /device:TPU:1 before, /device:TPU:32 now
where the time goes in v1:
time: 169 us
  Pallas kernels  69.2 us (41%)
  blocking collectives  46.4 us (27%)
  starting transfers between devices  39.5 us (23%)
  local copies, waits for them, and re-layouts  7.69 us (5%)
  other arithmetic  5.94 us (4%)
    pallas_call x1, Pallas kernels, stages(): call(inner_kernel, f32(LEVELS * 24, 128), 8, (win, pltpu.VMEM((LEVELS * 2...  38 us
    all_to_all x1, blocking collectives, stages(): parts = lax.all_to_all(parts, 'zh', 0, 0, tiled=True)  28.1 us
    pallas_call x1, Pallas kernels, stages(): call(outer_kernel, f32(32, 16, 128), 13, (win, pltpu.VMEM((LEVELS * 16, K...  26 us
    all_to_all x1, blocking collectives, stages(): arrived = lax.all_to_all(sent, ('y', 'lon', 'core'), 0, 0, tiled=True)  18.3 us
    ppermute x1, starting transfers between devices, stages(): lat_e = lax.ppermute(lat_e, LATF, lat_pairs(0))  11.8 us
    ppermute x3, starting transfers between devices, stages(): lax.ppermute(lax.dynamic_index_in_dim(legendre, place ^ d, 0, keepdims=Fa...  9.81 us
    ppermute x1, starting transfers between devices, stages(): cor_e = lax.ppermute(cor_e, LATF, lat_pairs(0))  9.1 us
    ppermute x1, starting transfers between devices, stages(): lon_o = lax.ppermute(lon_o, 'lon', lon_pairs(1))  4 us
  transfers between devices with their start and end apart: 9, of which 0 were waited for; matrix products, arithmetic and copies ran while one was open for 6% of the time, Pallas kernels for 38%

profile of v1, /device:TPU:32, one launch (start us, length us, event | category | flops | bytes accessed | tf_op | source)
XLA Modules:
  0.0 169.0 jit_solution(14024696576554419064)
XLA Ops:
  0.0 0.0 copy-start
  0.0 1.3 copy-done
  1.3 0.3 shard_map.82
  1.5 3.4 %collective-permute-start = (f32[40,128]{1,0:T(8,128)S(1)}, f32[40,128]{1,0:T(8,128)S(1)}, u32[]{:S(2)}, u32[]{:S(2)}) collective-permute-start(f32[40,128]{1,0:T(8,128)S(1)} %get-tuple-element.11), channel_id=1, source_target_pairs={{0,8},{8,0},{16,24},{24,16},{1,9},{9,1},{17,25},{25,17},{2,10},{10... | collective-permute-start | bytes 61448 | tf_op jit(solution)/shard_map/ppermute | solution.py:438
  5.0 4.0 %collective-permute-start.1 = (f32[40,128]{1,0:T(8,128)S(1)}, f32[40,128]{1,0:T(8,128)S(1)}, u32[]{:S(2)}, u32[]{:S(2)}) collective-permute-start(f32[40,128]{1,0:T(8,128)S(1)} %get-tuple-element.12), channel_id=1, source_target_pairs={{8,16},{16,8},{24,0},{0,24},{9,17},{17,9},{25,1},{1,25},{10,18},{1... | collective-permute-start | bytes 61448 | tf_op jit(solution)/shard_map/ppermute | solution.py:439
  9.0 0.0 copy-start.6
  9.0 0.0 copy-start.1
  9.0 0.0 copy-start.2
  9.0 0.0 copy-start.4
  9.0 3.3 %dynamic-slice_bitcast_fusion = (f32[160,1280]{1,0:T(8,128)}, f32[160,1280]{1,0:T(8,128)}, f32[160,1280]{1,0:T(8,128)}) fusion(f32[4,160,1280]{2,1,0:T(8,128)} %bitcast.7, s32[]{:T(128)S(6)} %select_n.50, s32[]{:T(128)S(6)} %select_n.49, s32[]{:T(128)S(6)} %select_n.48), kind=kLoop, calls=%fused_computation | loop fusion | bytes 4915212 | tf_op jit(solution)/shard_map/jit(dynamic_index_in_dim)/squeeze | solution.py:446
  12.3 4.9 %collective-permute-start.8 = (f32[160,1280]{1,0:T(8,128)}, f32[160,1280]{1,0:T(8,128)}, u32[]{:S(2)}, u32[]{:S(2)}) collective-permute-start(f32[160,1280]{1,0:T(8,128)} %get-tuple-element.17), channel_id=1, source_target_pairs={{0,384},{128,256},{256,128},{384,0},{1,385},{129,257},{257,129},{3... | collective-permute-start | bytes 2457608 | tf_op jit(solution)/shard_map/ppermute | solution.py:446
  17.2 2.5 %collective-permute-start.7 = (f32[160,1280]{1,0:T(8,128)}, f32[160,1280]{1,0:T(8,128)}, u32[]{:S(2)}, u32[]{:S(2)}) collective-permute-start(f32[160,1280]{1,0:T(8,128)} %get-tuple-element.18), channel_id=1, source_target_pairs={{0,256},{128,384},{256,0},{384,128},{1,257},{129,385},{257,1},{385... | collective-permute-start | bytes 2457608 | tf_op jit(solution)/shard_map/ppermute | solution.py:446
  19.8 2.4 %collective-permute-start.6 = (f32[160,1280]{1,0:T(8,128)}, f32[160,1280]{1,0:T(8,128)}, u32[]{:S(2)}, u32[]{:S(2)}) collective-permute-start(f32[160,1280]{1,0:T(8,128)} %get-tuple-element.19), channel_id=1, source_target_pairs={{0,128},{128,0},{256,384},{384,256},{1,129},{129,1},{257,385},{385... | collective-permute-start | bytes 2457608 | tf_op jit(solution)/shard_map/ppermute | solution.py:446
  22.1 0.6 fusion.12
  22.7 0.6 iota_shift-right-logical_fusion
  23.3 0.6 fusion.15
  23.9 0.6 iota_and_fusion.1
  24.5 0.0 collective-permute-done.lon_even
  24.5 0.0 collective-permute-done.1.lon_odd
  24.6 9.1 %collective-permute-start.4 = (f32[16,128]{1,0:T(8,128)S(1)}, f32[16,128]{1,0:T(8,128)S(1)}, u32[]{:S(2)}, u32[]{:S(2)}) collective-permute-start(f32[16,128]{1,0:T(8,128)S(1)} %get-tuple-element.15), channel_id=1, source_target_pairs={{0,32},{32,0},{1,33},{33,1},{2,34},{34,2},{3,35},{35,3},{4,36},{36... | collective-permute-start | bytes 24584 | tf_op jit(solution)/shard_map/ppermute | solution.py:441
  33.7 0.7 collective-permute-start.5
  34.3 0.6 compare_and_fusion
  34.9 0.0 copy-done.6
  34.9 0.1 broadcast_in_dim.7
  35.0 0.7 mul.29
  35.7 0.0 collective-permute-done.4.corner_even
  35.7 11.8 %collective-permute-start.2 = (f32[72,640]{1,0:T(8,128)S(1)}, f32[72,640]{1,0:T(8,128)S(1)}, u32[]{:S(2)}, u32[]{:S(2)}) collective-permute-start(f32[72,640]{1,0:T(8,128)S(1)} %get-tuple-element.13), channel_id=1, source_target_pairs={{0,32},{32,0},{1,33},{33,1},{2,34},{34,2},{3,35},{35,3},{4,36},{36... | collective-permute-start | bytes 552968 | tf_op jit(solution)/shard_map/ppermute | solution.py:436
  47.5 0.0 collective-permute-done.5.corner_odd
  47.5 0.7 collective-permute-start.3
  48.2 3.0 %fusion.6.table = f32[768,128]{1,0:T(8,128)S(1)} fusion(s32[128]{0:T(128)} %get-tuple-element.26, s32[128]{0:T(128)} %get-tuple-element.27, s32[128]{0:T(128)} %mul.29, s32[]{:T(128)S(6)} %mul.28, s32[768]{0:T(1024)} %get-tuple-element.20, s32[768]{0:T(1024)} %get-tuple-element.23, s32[768]{0:T(1024)} %get-tuple-element.21, s32[768]{0:T(1024)S(1)} %get-tuple-element.22, ...), kind=kLoop, calls=%fused_computation.13 | loop fusion | flops 2752512 | bytes 408708 | tf_op jit(solution)/shard_map/jit(_where)/select_n | solution.py:402
  51.2 0.0 copy-done.1
  51.2 0.0 copy-done.2
  51.2 0.0 copy-done.4
  51.2 0.0 copy-start.3
  51.2 1.3 copy-done.3
  52.5 1.1 copy-done.5
  53.6 38.0 %shard_map.84.inner = f32[288,128]{1,0:T(8,128)S(1)} custom-call(f32[1,12,40,640]{3,2,1,0:T(8,128)S(1)} %copy-done.1, s32[1,12,40,640]{3,2,1,0:T(8,128)S(1)} %copy-done.2, s32[1,12,40,640]{3,2,1,0:T(8,128)S(1)} %copy-done.3, bf16[1,12,40,640]{3,2,1,0:T(8,128)(2,1)S(1)} %copy-done.4, bf16[1,12,40,640]{3,2,1,0:T(8,128)(2,1)S(1)} %copy-done.5, ...), custom_call_target="tpu_custom_call" | custom-call | tf_op jit(solution)/shard_map/pallas_call | solution.py:451
  91.6 0.0 collective-permute-done.2.lat_even
  91.6 0.0 collective-permute-done.3.lat_odd
  91.6 26.0 %shard_map.85 = f32[32,16,128]{2,1,0:T(8,128)S(1)} custom-call(f32[1,12,40,640]{3,2,1,0:T(8,128)S(1)} %copy-done.1, s32[1,12,40,640]{3,2,1,0:T(8,128)S(1)} %copy-done.2, s32[1,12,40,640]{3,2,1,0:T(8,128)S(1)} %copy-done.3, bf16[1,12,40,640]{3,2,1,0:T(8,128)(2,1)S(1)} %copy-done.4, bf16[1,12,40,640]{3,2,1,0:T(8,128)(2,1)S(1)} %copy-done.5, ...), custom_call_target="tpu_custom_call" | custom-call | tf_op jit(solution)/shard_map/pallas_call | solution.py:454
  117.6 18.3 %all_to_all.10.arrived = f32[32,16,128]{2,1,0:T(8,128)S(1)} all-to-all(f32[32,16,128]{2,1,0:T(8,128)S(1)} %shard_map.85), channel_id=1, replica_groups=mesh['y'=4,'zh'=4,'lon'=4,'zl'=4,'core'=2] {'y','lon','core'}, dimensions={0} | all-to-all | bytes 524288 | tf_op jit(solution)/shard_map/all_to_all | solution.py:466
  135.9 0.0 collective-permute-done.8.from_3
  135.9 0.0 collective-permute-done.7.from_2
  135.9 0.0 collective-permute-done.6.from_1
  135.9 3.7 %shard_map.86 = f32[4,120,128]{2,1,0:T(8,128)S(1)} custom-call(s32[64]{0:T(128)S(1)} %copy-done.6, f32[32,16,128]{2,1,0:T(8,128)S(1)} %all_to_all.10.arrived, f32[4,160,1280]{2,1,0:T(8,128)} %bitcast.8, f32[160,1280]{1,0:T(8,128)} %collective-permute-done.6.from_1, f32[160,1280]{1,0:T(8,128)} %collective-permute-done.7.from_2, ...), custom_call_target="tpu_custom_call" | custom-call | tf_op jit(solution)/shard_map/pallas_call | solution.py:467
  139.6 28.1 %all_to_all.11.parts = f32[4,120,128]{2,1,0:T(8,128)S(1)} all-to-all(f32[4,120,128]{2,1,0:T(8,128)S(1)} %shard_map.86), channel_id=1, replica_groups=mesh['y'=4,'zh'=4,'lon'=4,'zl'=4,'core'=2] {'zh'}, dimensions={0} | all-to-all | bytes 491520 | tf_op jit(solution)/shard_map/all_to_all | solution.py:470
  167.7 0.0 copy-done.7
  167.7 1.2 shard_map.87
  (3 shorter events, 0.0 us)
Async XLA Ops:
  0.0 1.3 copy-start
  1.5 23.0 %collective-permute-start = (f32[40,128]{1,0:T(8,128)S(1)}, f32[40,128]{1,0:T(8,128)S(1)}, u32[]{:S(2)}, u32[]{:S(2)}) collective-permute-start(f32[40,128]{1,0:T(8,128)S(1)} %get-tuple-element.11), channel_id=1, source_target_pairs={{0,8},{8,0},{16,24},{24,16},{1,9},{9,1},{17,25},{25,17},{2,10},{10... | collective-permute-start | bytes 61448 | tf_op jit(solution)/shard_map/ppermute | solution.py:438
  5.0 19.6 %collective-permute-start.1 = (f32[40,128]{1,0:T(8,128)S(1)}, f32[40,128]{1,0:T(8,128)S(1)}, u32[]{:S(2)}, u32[]{:S(2)}) collective-permute-start(f32[40,128]{1,0:T(8,128)S(1)} %get-tuple-element.12), channel_id=1, source_target_pairs={{8,16},{16,8},{24,0},{0,24},{9,17},{17,9},{25,1},{1,25},{10,18},{1... | collective-permute-start | bytes 61448 | tf_op jit(solution)/shard_map/ppermute | solution.py:439
  9.0 25.9 %copy-start.6 = (s32[64]{0:T(128)S(1)}, s32[64]{0:T(128)}, u32[]{:S(2)}) copy-start(s32[64]{0:T(128)} %wave_map.1) | copy-start | bytes 772
  9.0 42.2 %copy-start.1 = (f32[1,12,40,640]{3,2,1,0:T(8,128)S(1)}, f32[1,12,40,640]{3,2,1,0:T(8,128)}, u32[]{:S(2)}) copy-start(f32[1,12,40,640]{3,2,1,0:T(8,128)} %field.5) | copy-start | bytes 3686404
  9.0 42.2 %copy-start.2 = (s32[1,12,40,640]{3,2,1,0:T(8,128)S(1)}, s32[1,12,40,640]{3,2,1,0:T(8,128)}, u32[]{:S(2)}) copy-start(s32[1,12,40,640]{3,2,1,0:T(8,128)} %row_shift.3) | copy-start | bytes 3686404
  9.0 42.2 %copy-start.4 = (bf16[1,12,40,640]{3,2,1,0:T(8,128)(2,1)S(1)}, bf16[1,12,40,640]{3,2,1,0:T(8,128)(2,1)}, u32[]{:S(2)}) copy-start(bf16[1,12,40,640]{3,2,1,0:T(8,128)(2,1)} %row_frac.3) | copy-start | bytes 1843204
  12.3 123.6 %collective-permute-start.8 = (f32[160,1280]{1,0:T(8,128)}, f32[160,1280]{1,0:T(8,128)}, u32[]{:S(2)}, u32[]{:S(2)}) collective-permute-start(f32[160,1280]{1,0:T(8,128)} %get-tuple-element.17), channel_id=1, source_target_pairs={{0,384},{128,256},{256,128},{384,0},{1,385},{129,257},{257,129},{3... | collective-permute-start | bytes 2457608 | tf_op jit(solution)/shard_map/ppermute | solution.py:446
  17.2 118.6 %collective-permute-start.7 = (f32[160,1280]{1,0:T(8,128)}, f32[160,1280]{1,0:T(8,128)}, u32[]{:S(2)}, u32[]{:S(2)}) collective-permute-start(f32[160,1280]{1,0:T(8,128)} %get-tuple-element.18), channel_id=1, source_target_pairs={{0,256},{128,384},{256,0},{384,128},{1,257},{129,385},{257,1},{385... | collective-permute-start | bytes 2457608 | tf_op jit(solution)/shard_map/ppermute | solution.py:446
  19.8 116.1 %collective-permute-start.6 = (f32[160,1280]{1,0:T(8,128)}, f32[160,1280]{1,0:T(8,128)}, u32[]{:S(2)}, u32[]{:S(2)}) collective-permute-start(f32[160,1280]{1,0:T(8,128)} %get-tuple-element.19), channel_id=1, source_target_pairs={{0,128},{128,0},{256,384},{384,256},{1,129},{129,1},{257,385},{385... | collective-permute-start | bytes 2457608 | tf_op jit(solution)/shard_map/ppermute | solution.py:446
  24.6 11.1 %collective-permute-start.4 = (f32[16,128]{1,0:T(8,128)S(1)}, f32[16,128]{1,0:T(8,128)S(1)}, u32[]{:S(2)}, u32[]{:S(2)}) collective-permute-start(f32[16,128]{1,0:T(8,128)S(1)} %get-tuple-element.15), channel_id=1, source_target_pairs={{0,32},{32,0},{1,33},{33,1},{2,34},{34,2},{3,35},{35,3},{4,36},{36... | collective-permute-start | bytes 24584 | tf_op jit(solution)/shard_map/ppermute | solution.py:441
  33.7 13.8 %collective-permute-start.5 = (f32[16,128]{1,0:T(8,128)S(1)}, f32[16,128]{1,0:T(8,128)S(1)}, u32[]{:S(2)}, u32[]{:S(2)}) collective-permute-start(f32[16,128]{1,0:T(8,128)S(1)} %get-tuple-element.16), channel_id=1, source_target_pairs={{32,64},{64,32},{33,65},{65,33},{34,66},{66,34},{35,67},{67,35},{3... | collective-permute-start | bytes 24584 | tf_op jit(solution)/shard_map/ppermute | solution.py:442
  35.7 55.9 %collective-permute-start.2 = (f32[72,640]{1,0:T(8,128)S(1)}, f32[72,640]{1,0:T(8,128)S(1)}, u32[]{:S(2)}, u32[]{:S(2)}) collective-permute-start(f32[72,640]{1,0:T(8,128)S(1)} %get-tuple-element.13), channel_id=1, source_target_pairs={{0,32},{32,0},{1,33},{33,1},{2,34},{34,2},{3,35},{35,3},{4,36},{36... | collective-permute-start | bytes 552968 | tf_op jit(solution)/shard_map/ppermute | solution.py:436
  47.5 44.1 %collective-permute-start.3 = (f32[72,640]{1,0:T(8,128)S(1)}, f32[72,640]{1,0:T(8,128)S(1)}, u32[]{:S(2)}, u32[]{:S(2)}) collective-permute-start(f32[72,640]{1,0:T(8,128)S(1)} %get-tuple-element.14), channel_id=1, source_target_pairs={{32,64},{64,32},{33,65},{65,33},{34,66},{66,34},{35,67},{67,35},{3... | collective-permute-start | bytes 552968 | tf_op jit(solution)/shard_map/ppermute | solution.py:437
  51.2 1.3 copy-start.3
  52.5 1.1 copy-start.5
  135.9 31.9 %copy-start.7 = (f32[6]{0:T(128)S(1)}, f32[6]{0:T(128)}, u32[]{:S(2)}) copy-start(f32[6]{0:T(128)} %helm.1) | copy-start | bytes 76

commit v2 on v1

--- a/solution.py
+++ b/solution.py
@@ -14,9 +14,6 @@
 TILES = 5
 DEG = 1280
 LON_TOTAL = 2560
-WIN = 107
-NWIN = 6
-KDIM = NWIN * 128
 VM = pltpu.CompilerParams(vmem_limit_bytes=48 * 1024 * 1024)
 LAT = ("y", "zh")
 LATF = ("y", "zh", "zl", "core")
@@ -48,14 +45,6 @@
 
 
 def edges_kernel(field, lat_even, lat_odd, lon_even, lon_odd):
-    lat = lat_index()
-    odd = lat % 2
-    for j in range(6):
-        at_even = jnp.where(odd == 0, 34 + j, j)
-        at_odd = jnp.where(odd == 0, j, jnp.where(lat == 15, 39 - j, 34 + j))
-        for l in range(LEVELS):
-            lat_even[pl.ds(6 * l + j, 1), :] = field[0, l, pl.ds(at_even, 1), :]
-            lat_odd[pl.ds(6 * l + j, 1), :] = field[0, l, pl.ds(at_odd, 1), :]
     lane = lane_iota()
     lon_par = lax.axis_index("lon") % 2
     for rt in range(TILES):
@@ -68,17 +57,32 @@
             right = jnp.where(here, roll(field[0, l, rows, 512:640], 8 * l - 122), right)
         lon_even[rows, :] = jnp.where(lon_par == 0, right, left)
         lon_odd[rows, :] = jnp.where(lon_par == 0, left, right)
-
-
-def corner_kernel(lon_even, lon_odd, to_even, to_odd):
+    for j, at_even, at_odd in edge_rows():
+        for l in range(LEVELS):
+            lat_even[pl.ds(6 * l + j, 1), :] = field[0, l, pl.ds(at_even, 1), :]
+            lat_odd[pl.ds(6 * l + j, 1), :] = field[0, l, pl.ds(at_odd, 1), :]
+    lat_even[72:80, :] = jnp.zeros((8, COLS), jnp.float32)
+    lat_odd[72:80, :] = jnp.zeros((8, COLS), jnp.float32)
+
+
+def edge_rows():
     lat = lat_index()
     odd = lat % 2
-    for r in range(8):
-        at_even = jnp.where(odd == 0, 32 + r, r)
-        at_odd = jnp.where(odd == 0, r, jnp.where(lat == 15, 39 - r, 32 + r))
+    for j in range(6):
+        at_even = jnp.where(odd == 0, 34 + j, j)
+        at_odd = jnp.where(odd == 0, j, jnp.where(lat == 15, 39 - j, 34 + j))
+        yield j, at_even, at_odd
+
+
+def corner_kernel(lon_even, lon_odd, _even, _odd, lat_even, lat_odd):
+    for j, at_even, at_odd in edge_rows():
         for k, ref in enumerate((lon_even, lon_odd)):
-            to_even[pl.ds(8 * k + r, 1), :] = ref[pl.ds(at_even, 1), :]
-            to_odd[pl.ds(8 * k + r, 1), :] = ref[pl.ds(at_odd, 1), :]
+            lat_even[72 + j : 73 + j, 128 * k : 128 * k + 128] = ref[pl.ds(at_even, 1), :]
+            lat_odd[72 + j : 73 + j, 128 * k : 128 * k + 128] = ref[pl.ds(at_odd, 1), :]
+    lat_even[78:80, :] = jnp.zeros((2, COLS), jnp.float32)
+    lat_odd[78:80, :] = jnp.zeros((2, COLS), jnp.float32)
+    for ref in (lat_even, lat_odd):
+        ref[72:78, 256:COLS] = jnp.zeros((6, COLS - 256), jnp.float32)
 
 
 def cubic(t):
@@ -95,23 +99,16 @@
     )
 
 
-def window(tiles, start, lane):
-    first, off = divmod(start, 128)
-    x = tiles[first]
-    if off:
-        if first + 1 < len(tiles):
-            x = jnp.where(lane >= off, x, tiles[first + 1])
-        x = roll(x, -off)
-    return x
-
-
-def take(x, index):
-    return jnp.take_along_axis(x, index, axis=1, mode="promise_in_bounds")
-
-
-def put_windows(win, row, tiles, lane):
-    for w in range(NWIN):
-        win[w, row : row + 8, :] = window(tiles, WIN * w + 123, lane)
+def put_shifted(sh, row, tiles, lane):
+    for t in range(TILES):
+        for k in range(12):
+            off = k - 5
+            x = tiles[t + 1]
+            if off > 0:
+                x = roll(jnp.where(lane >= off, x, tiles[t + 2]), -off)
+            elif off < 0:
+                x = roll(jnp.where(lane < 128 + off, x, tiles[t]), -off)
+            sh[k * TILES + t, row : row + 8, :] = x
 
 
 def lon_sides(lon_even, lon_odd, rows, lon_par):
@@ -124,23 +121,28 @@
     return pltpu.roll(x, shift, 1)
 
 
-def tile_points(win, at, w, shift_row, shift_col, frac_row, frac_col, lane):
-    def cut(ref_tiles):
-        return window(ref_tiles, WIN * w, lane)
-
-    rs = cut(shift_row)
-    cs = cut(shift_col)
-    wr = cubic(cut(frac_row))
-    wc = cubic(cut(frac_col))
-    first = jnp.minimum(cs + (lane + 4), 124)
-    index = [first, first + 1, first + 2, first + 3]
+def spread(shift, weights):
+    here = [shift == k for k in range(-4, 5)]
+    placed = []
+    for k in range(12):
+        value = None
+        for a in range(4):
+            if 0 <= k - a < 9:
+                value = jnp.where(here[k - a], weights[a], 0.0 if value is None else value)
+        placed.append(value)
+    return placed
+
+
+def tile_points(sh, at, t, rs, cs, row_frac, col_frac):
+    wc = spread(cs, cubic(col_frac))
     line = []
     for k in range(12):
-        src = win[w, at + k - 5 : at + k + 3, :]
-        acc = wc[0] * take(src, index[0])
-        for b in range(1, 4):
-            acc = acc + wc[b] * take(src, index[b])
+        acc = None
+        for o in range(12):
+            got = wc[o] * sh[o * TILES + t, at + k - 5 : at + k + 3, :]
+            acc = got if acc is None else acc + got
         line.append(acc)
+    wr = cubic(row_frac)
     u = rs + 4
     m = u >= 5
     line = [jnp.where(m, line[k + 5], line[k]) for k in range(7)] + [line[7]]
@@ -169,7 +171,7 @@
     for rt in row_tiles:
         left, right = lon_sides(lon_even, lon_odd, slice(8 * rt, 8 * rt + 8), lon_par)
         tiles = [dyn_roll(left, (250 - 8 * l) % 128)] + lane_tiles(field, l, rt) + [dyn_roll(right, (128 - 8 * l) % 128)]
-        put_windows(win, 8 + 8 * rt, tiles, lane)
+        put_shifted(win, 8 + 8 * rt, tiles, lane)
 
 
 def split(x):
@@ -187,10 +189,10 @@
     return dot(hi, t_hi) + (dot(lo, t_hi) + dot(hi, t_lo))
 
 
-def points_of(l, rt, win, row_shift, col_shift, row_frac, col_frac, lane, put):
+def points_of(l, rt, win, row_shift, col_shift, row_frac, col_frac, put):
     params = [lane_tiles(r, l, rt) for r in (row_shift, col_shift, row_frac, col_frac)]
-    for w in range(NWIN):
-        put(w, tile_points(win, 8 + 8 * rt, w, *params, lane))
+    for t in range(TILES):
+        put(t, tile_points(win, 8 + 8 * rt, t, *[p[t] for p in params]))
 
 
 def inner_kernel(field, row_shift, col_shift, row_frac, col_frac, lon_even, lon_odd, table, out, win, grid):
@@ -204,7 +206,7 @@
             def put(w, x, i=i):
                 grid[pl.ds(24 * l + 8 * i, 8), 128 * w : 128 * w + 128] = x
 
-            points_of(l, i + 1, win, row_shift, col_shift, row_frac, col_frac, lane, put)
+            points_of(l, i + 1, win, row_shift, col_shift, row_frac, col_frac, put)
         return carry
 
     lax.fori_loop(0, LEVELS, level, 0)
@@ -235,8 +237,6 @@
     lon_odd,
     lat_even,
     lat_odd,
-    corner_even,
-    corner_odd,
     table,
     inner,
     out,
@@ -250,42 +250,46 @@
     lon_par = lax.axis_index("lon") % 2
     lat_odd_place = lat_index() % 2
 
-    def place(before, after, corner_before, corner_after):
+    def place(before, after):
         for l in range(LEVELS):
             halo[0, l, 2:8, :] = before[6 * l : 6 * l + 6, :]
             halo[1, l, 0:6, :] = after[6 * l : 6 * l + 6, :]
-        side[0] = corner_before[...]
-        side[1] = corner_after[...]
+        for k in range(2):
+            side[0, k, 2:8, :] = before[72:78, 128 * k : 128 * k + 128]
+            side[1, k, 0:6, :] = after[72:78, 128 * k : 128 * k + 128]
 
     for l in range(LEVELS):
         halo[0, l, 0:2, :] = jnp.zeros((2, COLS), jnp.float32)
         halo[1, l, 6:8, :] = jnp.zeros((2, COLS), jnp.float32)
+    for k in range(2):
+        side[0, k, 0:2, :] = jnp.zeros((2, 128), jnp.float32)
+        side[1, k, 6:8, :] = jnp.zeros((2, 128), jnp.float32)
 
     @pl.when(lat_odd_place == 0)
     def _():
-        place(lat_odd, lat_even, corner_odd, corner_even)
+        place(lat_odd, lat_even)
 
     @pl.when(lat_odd_place == 1)
     def _():
-        place(lat_even, lat_odd, corner_even, corner_odd)
+        place(lat_even, lat_odd)
 
     def level(l, carry):
         main_rows(win, field, lon_even, lon_odd, l, (0, 1, 3, 4), lon_par, lane)
         for k, row in ((0, 0), (1, 48)):
-            even = side[k, 0:8, :]
-            odd = side[k, 8:16, :]
+            even = side[k, 0]
+            odd = side[k, 1]
             left = jnp.where(lon_par == 0, odd, even)
             right = jnp.where(lon_par == 0, even, odd)
             x = halo[k, l]
             tiles = [x[:, 128 * t : 128 * t + 128] for t in range(TILES)]
             tiles = [dyn_roll(left, (250 - 8 * l) % 128)] + tiles + [dyn_roll(right, (128 - 8 * l) % 128)]
-            put_windows(win, row, tiles, lane)
+            put_shifted(win, row, tiles, lane)
         for i, rt in enumerate((0, 4)):
 
             def put(w, x, i=i):
                 grid[pl.ds(16 * l + 8 * i, 8), 128 * w : 128 * w + 128] = x
 
-            points_of(l, rt, win, row_shift, col_shift, row_frac, col_frac, lane, put)
+            points_of(l, rt, win, row_shift, col_shift, row_frac, col_frac, put)
         return carry
 
     lax.fori_loop(0, LEVELS, level, 0)
@@ -391,15 +395,12 @@
 
 
 def zonal_table(wave_map):
-    k = lax.broadcasted_iota(jnp.int32, (KDIM, 128), 0)
-    lane = lax.broadcasted_iota(jnp.int32, (KDIM, 128), 1)
-    i = k % 128
-    col = k // 128 * WIN + i
-    valid = (i < WIN) & (col < COLS)
+    col = lax.broadcasted_iota(jnp.int32, (COLS, 128), 0)
+    lane = lax.broadcasted_iota(jnp.int32, (COLS, 128), 1)
     phase = (col + lax.axis_index("lon") * COLS) * jnp.repeat(wave_map, 2)[None, :] % LON_TOTAL
     phase = (phase + (lane % 2) * (LON_TOTAL // 4)) % LON_TOTAL
     angle = phase.astype(jnp.float32) * (2.0 * math.pi / LON_TOTAL)
-    return jnp.where(valid, jnp.cos(angle) / math.sqrt(LON_TOTAL), 0.0)
+    return jnp.cos(angle) / math.sqrt(LON_TOTAL)
 
 
 def lon_pairs(odd):
@@ -418,7 +419,7 @@
     return route
 
 
-def call(kernel, outs, count, scratch=(), smem_first=0):
+def call(kernel, outs, count, scratch=(), smem_first=0, alias={}):
     specs = [smem()] * smem_first + [vmem()] * (count - smem_first)
     return pl.pallas_call(
         kernel,
@@ -426,20 +427,38 @@
         in_specs=specs,
         out_specs=jax.tree.map(lambda _: vmem(), outs),
         scratch_shapes=list(scratch),
+        input_output_aliases=alias,
         compiler_params=VM,
     )
 
 
+def shifted():
+    return pltpu.VMEM((12 * TILES, 56, 128), jnp.float32)
+
+
+def run_inner(*args):
+    return call(inner_kernel, f32(LEVELS * 24, 128), 8, (shifted(), pltpu.VMEM((LEVELS * 24, COLS), jnp.float32)))(*args)
+
+
+def run_outer(*args):
+    scratch = (
+        shifted(),
+        pltpu.VMEM((LEVELS * 16, COLS), jnp.float32),
+        pltpu.VMEM((LEVELS * 16, 128), jnp.float32),
+        pltpu.VMEM((2, LEVELS, 8, COLS), jnp.float32),
+        pltpu.VMEM((2, 2, 8, 128), jnp.float32),
+    )
+    return call(outer_kernel, f32(32, 16, 128), 11, scratch)(*args)
+
+
 def stages(field, row_shift, col_shift, row_frac, col_frac, wave_map, legendre, helm_coef):
     grid_args = (field, row_shift, col_shift, row_frac, col_frac)
-    lat_e, lat_o, lon_e, lon_o = call(edges_kernel, (f32(72, COLS), f32(72, COLS), f32(ROWS, 128), f32(ROWS, 128)), 1)(field)
+    lat_e, lat_o, lon_e, lon_o = call(edges_kernel, (f32(80, COLS), f32(80, COLS), f32(ROWS, 128), f32(ROWS, 128)), 1)(field)
+    lon_e = lax.ppermute(lon_e, "lon", lon_pairs(0))
+    lon_o = lax.ppermute(lon_o, "lon", lon_pairs(1))
+    lat_e, lat_o = call(corner_kernel, (f32(80, COLS), f32(80, COLS)), 4, alias={2: 0, 3: 1})(lon_e, lon_o, lat_e, lat_o)
     lat_e = lax.ppermute(lat_e, LATF, lat_pairs(0))
     lat_o = lax.ppermute(lat_o, LATF, lat_pairs(1))
-    lon_e = lax.ppermute(lon_e, "lon", lon_pairs(0))
-    lon_o = lax.ppermute(lon_o, "lon", lon_pairs(1))
-    cor_e, cor_o = call(corner_kernel, (f32(16, 128), f32(16, 128)), 2)(lon_e, lon_o)
-    cor_e = lax.ppermute(cor_e, LATF, lat_pairs(0))
-    cor_o = lax.ppermute(cor_o, LATF, lat_pairs(1))
     legendre = legendre.reshape(4, 4 * ROWS, DEG)
     place = lax.axis_index("y")
     arrived_rows = [
@@ -447,22 +466,8 @@
         for d in (1, 2, 3)
     ]
     table = zonal_table(wave_map)
-    win = pltpu.VMEM((NWIN, 56, 128), jnp.float32)
-    inner = call(inner_kernel, f32(LEVELS * 24, 128), 8, (win, pltpu.VMEM((LEVELS * 24, KDIM), jnp.float32)))(
-        *grid_args, lon_e, lon_o, table
-    )
-    sent = call(
-        outer_kernel,
-        f32(32, 16, 128),
-        13,
-        (
-            win,
-            pltpu.VMEM((LEVELS * 16, KDIM), jnp.float32),
-            pltpu.VMEM((LEVELS * 16, 128), jnp.float32),
-            pltpu.VMEM((2, LEVELS, 8, COLS), jnp.float32),
-            pltpu.VMEM((2, 16, 128), jnp.float32),
-        ),
-    )(*grid_args, lon_e, lon_o, lat_e, lat_o, cor_e, cor_o, table, inner)
+    inner = run_inner(*grid_args, lon_e, lon_o, table)
+    sent = run_outer(*grid_args, lon_e, lon_o, lat_e, lat_o, table, inner)
     arrived = lax.all_to_all(sent, ("y", "lon", "core"), 0, 0, tiled=True)
     parts = call(legendre_kernel, f32(4, 120, 128), 6, (pltpu.VMEM((4, 32, 256), jnp.float32),), 1)(
         wave_map, arrived, legendre, *arrived_rows

time: 169 us -> 118 us (0.70)
  the two profiles are of different devices: /device:TPU:32 before, /device:TPU:1 now
where the time goes in v2:
time: 118 us
  blocking collectives  47.6 us (40%)
  Pallas kernels  31.6 us (27%)
  starting transfers between devices  26.3 us (22%)
  local copies, waits for them, and re-layouts  8.54 us (7%)
  other arithmetic  3.26 us (3%)
    all_to_all x1, blocking collectives, stages(): arrived = lax.all_to_all(sent, ('y', 'lon', 'core'), 0, 0, tiled=True)  24.6 us
    all_to_all x1, blocking collectives, stages(): parts = lax.all_to_all(parts, 'zh', 0, 0, tiled=True)  23 us
    pallas_call x1, Pallas kernels, run_inner(): call(inner_kernel, f32(LEVELS * 24, 128), 8, (shifted(), pltpu.VMEM((LEVE...  13.6 us
    pallas_call x1, Pallas kernels, run_outer(): return call(outer_kernel, f32(32, 16, 128), 11, scratch)(*args)  12.1 us
    ppermute x3, starting transfers between devices, stages(): lax.ppermute(lax.dynamic_index_in_dim(legendre, place ^ d, 0, keepdims=Fa...  9.17 us
    ppermute x1, starting transfers between devices, stages(): lat_e = lax.ppermute(lat_e, LATF, lat_pairs(0))  8.82 us
    ppermute x1, starting transfers between devices, stages(): lon_e = lax.ppermute(lon_e, 'lon', lon_pairs(0))  3.92 us
    pallas_call x1, Pallas kernels, stages(): call(legendre_kernel, f32(4, 120, 128), 6, (pltpu.VMEM((4, 32, 256), jnp....  3.76 us
  transfers between devices with their start and end apart: 7, of which 0 were waited for; matrix products, arithmetic and copies ran while one was open for 7% of the time, Pallas kernels for 22%

profile of v2, /device:TPU:1, one launch (start us, length us, event | category | flops | bytes accessed | tf_op | source)
XLA Modules:
  0.0 117.6 jit_solution(18123826551320300694)
XLA Ops:
  0.0 0.0 copy-start
  0.0 1.3 %copy-done = f32[1,12,40,640]{3,2,1,0:T(8,128)S(1)} copy-done((f32[1,12,40,640]{3,2,1,0:T(8,128)S(1)}, f32[1,12,40,640]{3,2,1,0:T(8,128)}, u32[]{:S(2)}) %copy-start) | copy-done | bytes 1228824
  1.3 0.9 shard_map.82
  2.2 3.9 %collective-permute-start = (f32[40,128]{1,0:T(8,128)}, f32[40,128]{1,0:T(8,128)S(1)}, u32[]{:S(2)}, u32[]{:S(2)}) collective-permute-start(f32[40,128]{1,0:T(8,128)} %get-tuple-element.11), channel_id=1, source_target_pairs={{0,8},{8,0},{16,24},{24,16},{1,9},{9,1},{17,25},{25,17},{2,10},{10... | collective-permute-start | bytes 61448 | tf_op jit(solution)/shard_map/ppermute | solution.py:457
  6.1 3.7 %collective-permute-start.1 = (f32[40,128]{1,0:T(8,128)S(1)}, f32[40,128]{1,0:T(8,128)S(1)}, u32[]{:S(2)}, u32[]{:S(2)}) collective-permute-start(f32[40,128]{1,0:T(8,128)S(1)} %get-tuple-element.12), channel_id=1, source_target_pairs={{8,16},{16,8},{24,0},{0,24},{9,17},{17,9},{25,1},{1,25},{10,18},{1... | collective-permute-start | bytes 61448 | tf_op jit(solution)/shard_map/ppermute | solution.py:458
  9.8 0.0 copy-start.6
  9.8 0.0 copy-start.1
  9.9 0.0 copy-start.2
  9.9 3.3 %dynamic-slice_bitcast_fusion = (f32[160,1280]{1,0:T(8,128)}, f32[160,1280]{1,0:T(8,128)}, f32[160,1280]{1,0:T(8,128)}) fusion(f32[4,160,1280]{2,1,0:T(8,128)} %bitcast.7, s32[]{:T(128)S(6)} %select_n.30, s32[]{:T(128)S(6)} %select_n.29, s32[]{:T(128)S(6)} %select_n.28), kind=kLoop, calls=%fused_computation | loop fusion | bytes 4915212 | tf_op jit(solution)/shard_map/jit(dynamic_index_in_dim)/squeeze | solution.py:465
  13.2 0.0 copy-start.4
  13.2 4.8 %collective-permute-start.6 = (f32[160,1280]{1,0:T(8,128)}, f32[160,1280]{1,0:T(8,128)}, u32[]{:S(2)}, u32[]{:S(2)}) collective-permute-start(f32[160,1280]{1,0:T(8,128)} %get-tuple-element.17), channel_id=1, source_target_pairs={{0,384},{128,256},{256,128},{384,0},{1,385},{129,257},{257,129},{3... | collective-permute-start | bytes 2457608 | tf_op jit(solution)/shard_map/ppermute | solution.py:465
  17.9 2.3 %collective-permute-start.5 = (f32[160,1280]{1,0:T(8,128)}, f32[160,1280]{1,0:T(8,128)}, u32[]{:S(2)}, u32[]{:S(2)}) collective-permute-start(f32[160,1280]{1,0:T(8,128)} %get-tuple-element.18), channel_id=1, source_target_pairs={{0,256},{128,384},{256,0},{384,128},{1,257},{129,385},{257,1},{385... | collective-permute-start | bytes 2457608 | tf_op jit(solution)/shard_map/ppermute | solution.py:465
  20.2 2.1 %collective-permute-start.4 = (f32[160,1280]{1,0:T(8,128)}, f32[160,1280]{1,0:T(8,128)}, u32[]{:S(2)}, u32[]{:S(2)}) collective-permute-start(f32[160,1280]{1,0:T(8,128)} %get-tuple-element.19), channel_id=1, source_target_pairs={{0,128},{128,0},{256,384},{384,256},{1,129},{129,1},{257,385},{385... | collective-permute-start | bytes 2457608 | tf_op jit(solution)/shard_map/ppermute | solution.py:465
  22.4 0.6 iota_and_fusion
  23.0 0.5 compare_and_fusion
  23.5 0.0 copy-done.6
  23.5 0.7 broadcast_in_dim.3
  24.2 0.9 mul.26
  25.1 0.0 collective-permute-done.lon_even
  25.1 0.0 collective-permute-done.1.lon_odd
  25.1 8.8 %collective-permute-start.2 = (f32[80,640]{1,0:T(8,128)S(1)}, f32[80,640]{1,0:T(8,128)S(1)}, u32[]{:S(2)}, u32[]{:S(2)}) collective-permute-start(f32[80,640]{1,0:T(8,128)S(1)} %get-tuple-element.15), channel_id=1, source_target_pairs={{0,32},{32,0},{1,33},{33,1},{2,34},{34,2},{3,35},{35,3},{4,36},{36... | collective-permute-start | bytes 614408 | tf_op jit(solution)/shard_map/ppermute | solution.py:460
  34.0 0.7 collective-permute-start.3
  34.6 2.2 %fusion.5.table = f32[640,128]{1,0:T(8,128)S(1)} fusion(s32[128]{0:T(128)} %get-tuple-element.20, s32[128]{0:T(128)} %get-tuple-element.21, s32[128]{0:T(128)S(1)} %mul.26, s32[640]{0:T(1024)S(1)} %iota_add_fusion, pred[128]{0:T(512)(128)(4,1)} %compare_and_fusion), kind=kLoop, calls=%fused_computation.10 | loop fusion | flops 1556480 | bytes 331904 | tf_op jit(solution)/shard_map/div | solution.py:403
  36.8 0.0 copy-done.1
  36.8 0.0 copy-done.2
  36.8 0.0 copy-done.4
  36.8 0.0 copy-start.3
  36.8 1.3 %copy-done.3 = s32[1,12,40,640]{3,2,1,0:T(8,128)S(1)} copy-done((s32[1,12,40,640]{3,2,1,0:T(8,128)S(1)}, s32[1,12,40,640]{3,2,1,0:T(8,128)}, u32[]{:S(2)}) %copy-start.3) | copy-done | bytes 1228824
  38.1 0.0 copy-start.5
  38.1 1.1 copy-done.5
  39.2 13.6 %shard_map.84.inner = f32[288,128]{1,0:T(8,128)S(1)} custom-call(f32[1,12,40,640]{3,2,1,0:T(8,128)S(1)} %copy-done.1, s32[1,12,40,640]{3,2,1,0:T(8,128)S(1)} %copy-done.2, s32[1,12,40,640]{3,2,1,0:T(8,128)S(1)} %copy-done.3, bf16[1,12,40,640]{3,2,1,0:T(8,128)(2,1)S(1)} %copy-done.4, bf16[1,12,40,640]{3,2,1,0:T(8,128)(2,1)S(1)} %copy-done.5, ...), custom_call_target="tpu_custom_call" | custom-call | tf_op jit(solution)/shard_map/pallas_call | solution.py:440
  52.8 0.0 collective-permute-done.2.lat_even
  52.9 0.0 collective-permute-done.3.lat_odd
  52.9 12.1 %shard_map.85 = f32[32,16,128]{2,1,0:T(8,128)S(1)} custom-call(f32[1,12,40,640]{3,2,1,0:T(8,128)S(1)} %copy-done.1, s32[1,12,40,640]{3,2,1,0:T(8,128)S(1)} %copy-done.2, s32[1,12,40,640]{3,2,1,0:T(8,128)S(1)} %copy-done.3, bf16[1,12,40,640]{3,2,1,0:T(8,128)(2,1)S(1)} %copy-done.4, bf16[1,12,40,640]{3,2,1,0:T(8,128)(2,1)S(1)} %copy-done.5, ...), custom_call_target="tpu_custom_call" | custom-call | tf_op jit(solution)/shard_map/pallas_call | solution.py:451
  64.9 24.6 %all_to_all.10.arrived = f32[32,16,128]{2,1,0:T(8,128)S(1)} all-to-all(f32[32,16,128]{2,1,0:T(8,128)S(1)} %shard_map.85), channel_id=1, replica_groups=mesh['y'=4,'zh'=4,'lon'=4,'zl'=4,'core'=2] {'y','lon','core'}, dimensions={0} | all-to-all | bytes 524288 | tf_op jit(solution)/shard_map/all_to_all | solution.py:471
  89.5 0.0 copy-start.7
  89.5 0.0 collective-permute-done.6.from_3
  89.5 0.0 collective-permute-done.5.from_2
  89.5 0.0 collective-permute-done.4.from_1
  89.6 3.8 %shard_map.86 = f32[4,120,128]{2,1,0:T(8,128)S(1)} custom-call(s32[64]{0:T(128)S(1)} %copy-done.6, f32[32,16,128]{2,1,0:T(8,128)S(1)} %all_to_all.10.arrived, f32[4,160,1280]{2,1,0:T(8,128)} %bitcast.8, f32[160,1280]{1,0:T(8,128)} %collective-permute-done.4.from_1, f32[160,1280]{1,0:T(8,128)} %collective-permute-done.5.from_2, ...), custom_call_target="tpu_custom_call" | custom-call | tf_op jit(solution)/shard_map/pallas_call | solution.py:472
  93.3 23.0 %all_to_all.11.parts = f32[4,120,128]{2,1,0:T(8,128)S(1)} all-to-all(f32[4,120,128]{2,1,0:T(8,128)S(1)} %shard_map.86), channel_id=1, replica_groups=mesh['y'=4,'zh'=4,'lon'=4,'zl'=4,'core'=2] {'zh'}, dimensions={0} | all-to-all | bytes 491520 | tf_op jit(solution)/shard_map/all_to_all | solution.py:475
  116.3 0.0 copy-done.7
  116.3 1.2 %shard_map.87 = f32[6,1,1,2560]{3,2,1,0:T(1,128)} custom-call(f32[6]{0:T(128)S(1)} %copy-done.7, f32[4,120,128]{2,1,0:T(8,128)S(1)} %all_to_all.11.parts), custom_call_target="tpu_custom_call" | custom-call | tf_op jit(solution)/shard_map/pallas_call | solution.py:476
  (2 shorter events, 0.0 us)
Async XLA Ops:
  0.0 1.3 %copy-start = (f32[1,12,40,640]{3,2,1,0:T(8,128)S(1)}, f32[1,12,40,640]{3,2,1,0:T(8,128)}, u32[]{:S(2)}) copy-start(f32[1,12,40,640]{3,2,1,0:T(8,128)} %field.5) | copy-start | bytes 3686404
  2.2 22.9 %collective-permute-start = (f32[40,128]{1,0:T(8,128)}, f32[40,128]{1,0:T(8,128)S(1)}, u32[]{:S(2)}, u32[]{:S(2)}) collective-permute-start(f32[40,128]{1,0:T(8,128)} %get-tuple-element.11), channel_id=1, source_target_pairs={{0,8},{8,0},{16,24},{24,16},{1,9},{9,1},{17,25},{25,17},{2,10},{10... | collective-permute-start | bytes 61448 | tf_op jit(solution)/shard_map/ppermute | solution.py:457
  6.1 19.0 %collective-permute-start.1 = (f32[40,128]{1,0:T(8,128)S(1)}, f32[40,128]{1,0:T(8,128)S(1)}, u32[]{:S(2)}, u32[]{:S(2)}) collective-permute-start(f32[40,128]{1,0:T(8,128)S(1)} %get-tuple-element.12), channel_id=1, source_target_pairs={{8,16},{16,8},{24,0},{0,24},{9,17},{17,9},{25,1},{1,25},{10,18},{1... | collective-permute-start | bytes 61448 | tf_op jit(solution)/shard_map/ppermute | solution.py:458
  9.8 13.6 %copy-start.6 = (s32[64]{0:T(128)S(1)}, s32[64]{0:T(128)}, u32[]{:S(2)}) copy-start(s32[64]{0:T(128)} %wave_map.1) | copy-start | bytes 772
  9.8 26.9 %copy-start.1 = (f32[1,12,40,640]{3,2,1,0:T(8,128)S(1)}, f32[1,12,40,640]{3,2,1,0:T(8,128)}, u32[]{:S(2)}) copy-start(f32[1,12,40,640]{3,2,1,0:T(8,128)} %field.5) | copy-start | bytes 3686404
  9.9 26.9 %copy-start.2 = (s32[1,12,40,640]{3,2,1,0:T(8,128)S(1)}, s32[1,12,40,640]{3,2,1,0:T(8,128)}, u32[]{:S(2)}) copy-start(s32[1,12,40,640]{3,2,1,0:T(8,128)} %row_shift.3) | copy-start | bytes 3686404
  13.2 23.6 %copy-start.4 = (bf16[1,12,40,640]{3,2,1,0:T(8,128)(2,1)S(1)}, bf16[1,12,40,640]{3,2,1,0:T(8,128)(2,1)}, u32[]{:S(2)}) copy-start(bf16[1,12,40,640]{3,2,1,0:T(8,128)(2,1)} %row_frac.3) | copy-start | bytes 1843204
  13.2 76.4 %collective-permute-start.6 = (f32[160,1280]{1,0:T(8,128)}, f32[160,1280]{1,0:T(8,128)}, u32[]{:S(2)}, u32[]{:S(2)}) collective-permute-start(f32[160,1280]{1,0:T(8,128)} %get-tuple-element.17), channel_id=1, source_target_pairs={{0,384},{128,256},{256,128},{384,0},{1,385},{129,257},{257,129},{3... | collective-permute-start | bytes 2457608 | tf_op jit(solution)/shard_map/ppermute | solution.py:465
  17.9 71.6 %collective-permute-start.5 = (f32[160,1280]{1,0:T(8,128)}, f32[160,1280]{1,0:T(8,128)}, u32[]{:S(2)}, u32[]{:S(2)}) collective-permute-start(f32[160,1280]{1,0:T(8,128)} %get-tuple-element.18), channel_id=1, source_target_pairs={{0,256},{128,384},{256,0},{384,128},{1,257},{129,385},{257,1},{385... | collective-permute-start | bytes 2457608 | tf_op jit(solution)/shard_map/ppermute | solution.py:465
  20.2 69.3 %collective-permute-start.4 = (f32[160,1280]{1,0:T(8,128)}, f32[160,1280]{1,0:T(8,128)}, u32[]{:S(2)}, u32[]{:S(2)}) collective-permute-start(f32[160,1280]{1,0:T(8,128)} %get-tuple-element.19), channel_id=1, source_target_pairs={{0,128},{128,0},{256,384},{384,256},{1,129},{129,1},{257,385},{385... | collective-permute-start | bytes 2457608 | tf_op jit(solution)/shard_map/ppermute | solution.py:465
  25.1 27.7 %collective-permute-start.2 = (f32[80,640]{1,0:T(8,128)S(1)}, f32[80,640]{1,0:T(8,128)S(1)}, u32[]{:S(2)}, u32[]{:S(2)}) collective-permute-start(f32[80,640]{1,0:T(8,128)S(1)} %get-tuple-element.15), channel_id=1, source_target_pairs={{0,32},{32,0},{1,33},{33,1},{2,34},{34,2},{3,35},{35,3},{4,36},{36... | collective-permute-start | bytes 614408 | tf_op jit(solution)/shard_map/ppermute | solution.py:460
  34.0 18.9 %collective-permute-start.3 = (f32[80,640]{1,0:T(8,128)S(1)}, f32[80,640]{1,0:T(8,128)S(1)}, u32[]{:S(2)}, u32[]{:S(2)}) collective-permute-start(f32[80,640]{1,0:T(8,128)S(1)} %get-tuple-element.16), channel_id=1, source_target_pairs={{32,64},{64,32},{33,65},{65,33},{34,66},{66,34},{35,67},{67,35},{3... | collective-permute-start | bytes 614408 | tf_op jit(solution)/shard_map/ppermute | solution.py:461
  36.8 1.3 %copy-start.3 = (s32[1,12,40,640]{3,2,1,0:T(8,128)S(1)}, s32[1,12,40,640]{3,2,1,0:T(8,128)}, u32[]{:S(2)}) copy-start(s32[1,12,40,640]{3,2,1,0:T(8,128)} %col_shift.3) | copy-start | bytes 3686404
  38.1 1.1 copy-start.5
  89.5 26.8 %copy-start.7 = (f32[6]{0:T(128)S(1)}, f32[6]{0:T(128)}, u32[]{:S(2)}) copy-start(f32[6]{0:T(128)} %helm.1) | copy-start | bytes 76

commit v3 on v2

--- a/solution.py
+++ b/solution.py
@@ -44,7 +44,7 @@
     return lax.axis_index("y") * 4 + lax.axis_index("zh")
 
 
-def edges_kernel(field, lat_even, lat_odd, lon_even, lon_odd):
+def edges_kernel(field, lon_even, lon_odd):
     lane = lane_iota()
     lon_par = lax.axis_index("lon") % 2
     for rt in range(TILES):
@@ -57,32 +57,23 @@
             right = jnp.where(here, roll(field[0, l, rows, 512:640], 8 * l - 122), right)
         lon_even[rows, :] = jnp.where(lon_par == 0, right, left)
         lon_odd[rows, :] = jnp.where(lon_par == 0, left, right)
-    for j, at_even, at_odd in edge_rows():
-        for l in range(LEVELS):
-            lat_even[pl.ds(6 * l + j, 1), :] = field[0, l, pl.ds(at_even, 1), :]
-            lat_odd[pl.ds(6 * l + j, 1), :] = field[0, l, pl.ds(at_odd, 1), :]
-    lat_even[72:80, :] = jnp.zeros((8, COLS), jnp.float32)
-    lat_odd[72:80, :] = jnp.zeros((8, COLS), jnp.float32)
-
-
-def edge_rows():
-    lat = lat_index()
-    odd = lat % 2
-    for j in range(6):
-        at_even = jnp.where(odd == 0, 34 + j, j)
-        at_odd = jnp.where(odd == 0, j, jnp.where(lat == 15, 39 - j, 34 + j))
-        yield j, at_even, at_odd
-
-
-def corner_kernel(lon_even, lon_odd, _even, _odd, lat_even, lat_odd):
-    for j, at_even, at_odd in edge_rows():
-        for k, ref in enumerate((lon_even, lon_odd)):
-            lat_even[72 + j : 73 + j, 128 * k : 128 * k + 128] = ref[pl.ds(at_even, 1), :]
-            lat_odd[72 + j : 73 + j, 128 * k : 128 * k + 128] = ref[pl.ds(at_odd, 1), :]
-    lat_even[78:80, :] = jnp.zeros((2, COLS), jnp.float32)
-    lat_odd[78:80, :] = jnp.zeros((2, COLS), jnp.float32)
-    for ref in (lat_even, lat_odd):
-        ref[72:78, 256:COLS] = jnp.zeros((6, COLS - 256), jnp.float32)
+
+
+def corner_kernel(field, lon_even, lon_odd, _shift, _frac, up, down, mirror):
+    for l in range(LEVELS):
+        up[5 * l : 5 * l + 5, :] = field[0, l, 35:40, :]
+        down[6 * l : 6 * l + 6, :] = field[0, l, 0:6, :]
+        for j in range(6):
+            mirror[6 * l + j : 6 * l + j + 1, :] = field[0, l, 39 - j : 40 - j, :]
+    up[60:72, :] = jnp.zeros((12, COLS), jnp.float32)
+    down[72:80, :] = jnp.zeros((8, COLS), jnp.float32)
+    mirror[72:80, :] = jnp.zeros((8, COLS), jnp.float32)
+    for k, ref in enumerate((lon_even, lon_odd)):
+        at = slice(128 * k, 128 * k + 128)
+        up[60:65, at] = ref[35:40, :]
+        down[72:78, at] = ref[0:6, :]
+        for j in range(6):
+            mirror[72 + j : 73 + j, at] = ref[39 - j : 40 - j, :]
 
 
 def cubic(t):
@@ -121,27 +112,38 @@
     return pltpu.roll(x, shift, 1)
 
 
-def spread(shift, weights):
-    here = [shift == k for k in range(-4, 5)]
-    placed = []
-    for k in range(12):
+def spread(shift, weights, offsets=range(12)):
+    placed = {}
+    for k in offsets:
         value = None
         for a in range(4):
             if 0 <= k - a < 9:
-                value = jnp.where(here[k - a], weights[a], 0.0 if value is None else value)
-        placed.append(value)
+                value = jnp.where(shift == k - a - 4, weights[a], 0.0 if value is None else value)
+        placed[k] = value
     return placed
+
+
+def line_of(sh, at, t, wc, k):
+    acc = None
+    for o in range(12):
+        got = wc[o] * sh[o * TILES + t, at + k - 5 : at + k + 3, :]
+        acc = got if acc is None else acc + got
+    return acc
+
+
+def some_rows(sh, at, t, rs, cs, row_frac, col_frac, offsets):
+    wc = spread(cs, cubic(col_frac))
+    wr = spread(rs, cubic(row_frac), offsets)
+    total = None
+    for k in offsets:
+        part = wr[k] * line_of(sh, at, t, wc, k)
+        total = part if total is None else total + part
+    return total
 
 
 def tile_points(sh, at, t, rs, cs, row_frac, col_frac):
     wc = spread(cs, cubic(col_frac))
-    line = []
-    for k in range(12):
-        acc = None
-        for o in range(12):
-            got = wc[o] * sh[o * TILES + t, at + k - 5 : at + k + 3, :]
-            acc = got if acc is None else acc + got
-        line.append(acc)
+    line = [line_of(sh, at, t, wc, k) for k in range(12)]
     wr = cubic(row_frac)
     u = rs + 4
     m = u >= 5
@@ -161,7 +163,10 @@
 
 
 def lane_tiles(ref, l, rt):
-    x = ref[0, l, pl.ds(8 * rt, 8), :]
+    if len(ref.shape) == 2:
+        x = ref[pl.ds(16 * l + 2 * rt, 8), :]
+    else:
+        x = ref[0, l, pl.ds(8 * rt, 8), :]
     if x.dtype == jnp.bfloat16:
         x = x.astype(jnp.float32)
     return [x[:, 128 * t : 128 * t + 128] for t in range(TILES)]
@@ -189,17 +194,23 @@
     return dot(hi, t_hi) + (dot(lo, t_hi) + dot(hi, t_lo))
 
 
-def points_of(l, rt, win, row_shift, col_shift, row_frac, col_frac, put):
+def points_of(l, rt, win, row_shift, col_shift, row_frac, col_frac, put, offsets=None):
     params = [lane_tiles(r, l, rt) for r in (row_shift, col_shift, row_frac, col_frac)]
     for t in range(TILES):
-        put(t, tile_points(win, 8 + 8 * rt, t, *[p[t] for p in params]))
-
-
-def inner_kernel(field, row_shift, col_shift, row_frac, col_frac, lon_even, lon_odd, table, out, win, grid):
+        here = [p[t] for p in params]
+        if offsets is None:
+            put(t, tile_points(win, 8 + 8 * rt, t, *here))
+        else:
+            put(t, some_rows(win, 8 + 8 * rt, t, *here, offsets))
+
+
+def inner_kernel(field, row_shift, col_shift, row_frac, col_frac, lon_even, lon_odd, table, out, partial, edge_shift, win, grid):
     lane = lane_iota()
     lon_par = lax.axis_index("lon") % 2
 
     def level(l, carry):
+        for i, rt in enumerate((0, 4)):
+            edge_shift[pl.ds(16 * l + 8 * i, 8), :] = col_shift[0, l, 8 * rt : 8 * rt + 8, :]
         main_rows(win, field, lon_even, lon_odd, l, range(TILES), lon_par, lane)
         for i in range(3):
 
@@ -207,6 +218,12 @@
                 grid[pl.ds(24 * l + 8 * i, 8), 128 * w : 128 * w + 128] = x
 
             points_of(l, i + 1, win, row_shift, col_shift, row_frac, col_frac, put)
+        for i, rt, offsets in ((0, 0, range(5, 12)), (1, 4, range(0, 6))):
+
+            def put_part(w, x, i=i):
+                partial[pl.ds(16 * l + 8 * i, 8), 128 * w : 128 * w + 128] = x
+
+            points_of(l, rt, win, row_shift, col_shift, row_frac, col_frac, put_part, offsets)
         return carry
 
     lax.fori_loop(0, LEVELS, level, 0)
@@ -235,10 +252,12 @@
     col_frac,
     lon_even,
     lon_odd,
-    lat_even,
-    lat_odd,
+    up,
+    down,
+    mirror,
     table,
     inner,
+    partial,
     out,
     win,
     grid,
@@ -248,33 +267,32 @@
 ):
     lane = lane_iota()
     lon_par = lax.axis_index("lon") % 2
-    lat_odd_place = lat_index() % 2
-
-    def place(before, after):
+
+    for l in range(LEVELS):
+        halo[0, l, 0:3, :] = jnp.zeros((3, COLS), jnp.float32)
+        halo[0, l, 3:8, :] = up[5 * l : 5 * l + 5, :]
+        halo[1, l, 6:8, :] = jnp.zeros((2, COLS), jnp.float32)
+    for k in range(2):
+        side[0, k, 0:3, :] = jnp.zeros((3, 128), jnp.float32)
+        side[0, k, 3:8, :] = up[60:65, 128 * k : 128 * k + 128]
+        side[1, k, 6:8, :] = jnp.zeros((2, 128), jnp.float32)
+
+    def place(after):
         for l in range(LEVELS):
-            halo[0, l, 2:8, :] = before[6 * l : 6 * l + 6, :]
             halo[1, l, 0:6, :] = after[6 * l : 6 * l + 6, :]
         for k in range(2):
-            side[0, k, 2:8, :] = before[72:78, 128 * k : 128 * k + 128]
             side[1, k, 0:6, :] = after[72:78, 128 * k : 128 * k + 128]
 
-    for l in range(LEVELS):
-        halo[0, l, 0:2, :] = jnp.zeros((2, COLS), jnp.float32)
-        halo[1, l, 6:8, :] = jnp.zeros((2, COLS), jnp.float32)
-    for k in range(2):
-        side[0, k, 0:2, :] = jnp.zeros((2, 128), jnp.float32)
-        side[1, k, 6:8, :] = jnp.zeros((2, 128), jnp.float32)
-
-    @pl.when(lat_odd_place == 0)
+    @pl.when(lat_index() < 15)
     def _():
-        place(lat_odd, lat_even)
-
-    @pl.when(lat_odd_place == 1)
+        place(down)
+
+    @pl.when(lat_index() == 15)
     def _():
-        place(lat_even, lat_odd)
+        place(mirror)
 
     def level(l, carry):
-        main_rows(win, field, lon_even, lon_odd, l, (0, 1, 3, 4), lon_par, lane)
+        main_rows(win, field, lon_even, lon_odd, l, (0, 4), lon_par, lane)
         for k, row in ((0, 0), (1, 48)):
             even = side[k, 0]
             odd = side[k, 1]
@@ -284,12 +302,14 @@
             tiles = [x[:, 128 * t : 128 * t + 128] for t in range(TILES)]
             tiles = [dyn_roll(left, (250 - 8 * l) % 128)] + tiles + [dyn_roll(right, (128 - 8 * l) % 128)]
             put_shifted(win, row, tiles, lane)
-        for i, rt in enumerate((0, 4)):
+        for i, rt, offsets in ((0, 0, range(0, 5)), (1, 4, range(6, 12))):
 
             def put(w, x, i=i):
-                grid[pl.ds(16 * l + 8 * i, 8), 128 * w : 128 * w + 128] = x
-
-            points_of(l, rt, win, row_shift, col_shift, row_frac, col_frac, put)
+                at = pl.ds(16 * l + 8 * i, 8)
+                lanes = slice(128 * w, 128 * w + 128)
+                grid[at, lanes] = partial[at, lanes] + x
+
+            points_of(l, rt, win, row_shift, col_shift, row_frac, col_frac, put, offsets)
         return carry
 
     lax.fori_loop(0, LEVELS, level, 0)
@@ -312,18 +332,22 @@
                 out[y * 8 + lon * 2 + core, 8 * v : 8 * v + 8, :] = block[d]
 
 
-def legendre_kernel(wave_map, arrived, legendre, from_1, from_2, from_3, out, lhs):
+def legendre_kernel(wave_map, arrived, legendre, near, far, other, out, to_1, to_2, to_3, lhs, sums_out, mine, sem):
     lane = lane_iota()
     place = lax.axis_index("y")
+    core = lax.axis_index("core")
+    fetch = pltpu.make_async_copy(legendre.at[place], mine, sem)
+    fetch.start()
+    holder = [place, place ^ (1 + core), place ^ (2 - core), place ^ 3]
     pieces = []
     for v in range(2):
         half = {}
         for y in range(4):
             sums = []
-            for core in range(2):
-                x = arrived[(place ^ y) * 8 + core, 8 * v : 8 * v + 8, :]
+            for hemisphere in range(2):
+                x = arrived[holder[y] * 8 + hemisphere, 8 * v : 8 * v + 8, :]
                 for lon in range(1, 4):
-                    x = x + arrived[(place ^ y) * 8 + lon * 2 + core, 8 * v : 8 * v + 8, :]
+                    x = x + arrived[holder[y] * 8 + lon * 2 + hemisphere, 8 * v : 8 * v + 8, :]
                 sums.append(x)
             half[0, y] = sums[0] + sums[1]
             half[1, y] = sums[0] - sums[1]
@@ -349,27 +373,34 @@
     slot = lax.axis_index("lon") * 16 + lax.axis_index("y") * 4
     degree = lax.broadcasted_iota(jnp.int32, (16, DEG), 1)
     low = lax.broadcasted_iota(jnp.int32, (8, 128), 0) < 4
-    for s in range(4):
+    fetch.wait()
+    for i in range(4):
+        s = 2 * core + i if i < 2 else 2 * (1 - core) + i - 2
+        to = s ^ lax.axis_index("zh")
         wave = wave_map[slot + s]
         a_hi, a_lo = split(lhs[s][:, 0:160])
         rows = []
         for rt in range(TILES):
-            at = slice(40 * s + 8 * rt, 40 * s + 8 * rt + 8)
-            rows += [legendre[place, at, :], from_1[at, :], from_2[at, :], from_3[at, :]]
+            whole = pl.ds(pl.multiple_of(40 * s + 8 * rt, 8), 8)
+            at = 40 * (i % 2) + 8 * rt
+            rows += [mine[whole, :], near[whole, :], other[whole, :]]
+            rows.append(far[at : at + 8, :] if i < 2 else other[160 + at : 168 + at, :])
         b_hi, b_lo = split(jnp.concatenate(rows, axis=0))
         sums = dot(a_hi, b_hi) + (dot(a_lo, b_hi) + dot(a_hi, b_lo))
         picked = jnp.where((degree + wave) % 2 == 0, sums[0:16], sums[16:32])
         picked = jnp.where(degree >= wave, picked, 0.0)
         for j in range(10):
-            out[s, 8 * j : 8 * j + 8, :] = picked[0:8, 128 * j : 128 * j + 128]
+            sums_out[to, 8 * j : 8 * j + 8, :] = picked[0:8, 128 * j : 128 * j + 128]
         for j in range(0, 10, 2):
             a = picked[8:16, 128 * j : 128 * j + 128]
             b = picked[8:16, 128 * j + 128 : 128 * j + 256]
-            out[s, 80 + 4 * j : 88 + 4 * j, :] = jnp.where(low, a, pltpu.roll(b, 4, 0))
-
-
-def finish_kernel(helm, parts, out):
-    total = parts[0] + parts[1] + (parts[2] + parts[3])
+            sums_out[to, 80 + 4 * j : 88 + 4 * j, :] = jnp.where(low, a, pltpu.roll(b, 4, 0))
+    for d, ref in enumerate((out, to_1, to_2, to_3)):
+        ref[...] = sums_out[d]
+
+
+def finish_kernel(helm, own, part_1, part_2, part_3, out):
+    total = own[...] + part_1[...] + (part_2[...] + part_3[...])
     row = lax.broadcasted_iota(jnp.int32, (8, 128), 0)
     lane = lane_iota()
 
@@ -395,39 +426,45 @@
 
 
 def zonal_table(wave_map):
-    col = lax.broadcasted_iota(jnp.int32, (COLS, 128), 0)
-    lane = lax.broadcasted_iota(jnp.int32, (COLS, 128), 1)
-    phase = (col + lax.axis_index("lon") * COLS) * jnp.repeat(wave_map, 2)[None, :] % LON_TOTAL
-    phase = (phase + (lane % 2) * (LON_TOTAL // 4)) % LON_TOTAL
-    angle = phase.astype(jnp.float32) * (2.0 * math.pi / LON_TOTAL)
-    return jnp.cos(angle) / math.sqrt(LON_TOTAL)
+    slot = lax.broadcasted_iota(jnp.int32, (64, 128), 0)
+    pair = lax.broadcasted_iota(jnp.int32, (64, 128), 1) // 2
+    wave = jnp.sum(jnp.where(slot == pair, wave_map[:, None], 0), axis=0)[None, :]
+
+    def angle(col, quarter):
+        phase = (col * wave + quarter * (LON_TOTAL // 4)) % LON_TOTAL
+        return phase.astype(jnp.float32) * (2.0 * math.pi / LON_TOTAL)
+
+    lane = lax.broadcasted_iota(jnp.int32, (80, 128), 1)
+    coarse = angle(lax.axis_index("lon") * COLS + 8 * lax.broadcasted_iota(jnp.int32, (80, 128), 0), lane % 2)
+    fine = angle(lax.broadcasted_iota(jnp.int32, (8, 128), 0), 0)
+    scale = 1.0 / math.sqrt(LON_TOTAL)
+    c, d = jnp.cos(coarse) * scale, jnp.sin(coarse) * scale
+    table = c[:, None, :] * jnp.cos(fine)[None] - d[:, None, :] * jnp.sin(fine)[None]
+    return table.reshape(COLS, 128)
 
 
 def lon_pairs(odd):
     return [r for i in range(odd, 4, 2) for r in ((i, (i + 1) % 4), ((i + 1) % 4, i))]
 
 
-def lat_pairs(odd):
-    route = []
-    for i in range(odd, 15, 2):
-        for f in range(8):
-            low, high = i * 8 + f, (i + 1) * 8 + f
-            route += [(low, high), (high, low)]
-    if odd:
-        for f in range(8):
-            route.append((15 * 8 + f, 15 * 8 + (f ^ 1)))
-    return route
-
-
-def call(kernel, outs, count, scratch=(), smem_first=0, alias={}):
+def lat_shift(step):
+    return [(i * 8 + f, (i + step) * 8 + f) for i in range(16) for f in range(8) if 0 <= i + step < 16]
+
+
+def equator():
+    return [(15 * 8 + f, 15 * 8 + (f ^ 1)) for f in range(8)]
+
+
+def call(kernel, outs, count, scratch=(), smem_first=0, whole=None):
     specs = [smem()] * smem_first + [vmem()] * (count - smem_first)
+    if whole is not None:
+        specs[whole] = pl.BlockSpec(memory_space=pl.ANY)
     return pl.pallas_call(
         kernel,
         out_shape=outs,
         in_specs=specs,
         out_specs=jax.tree.map(lambda _: vmem(), outs),
         scratch_shapes=list(scratch),
-        input_output_aliases=alias,
         compiler_params=VM,
     )
 
@@ -437,7 +474,8 @@
 
 
 def run_inner(*args):
-    return call(inner_kernel, f32(LEVELS * 24, 128), 8, (shifted(), pltpu.VMEM((LEVELS * 24, COLS), jnp.float32)))(*args)
+    outs = (f32(LEVELS * 24, 128), f32(LEVELS * 16, COLS), jax.ShapeDtypeStruct((LEVELS * 16, COLS), jnp.int32))
+    return call(inner_kernel, outs, 8, (shifted(), pltpu.VMEM((LEVELS * 24, COLS), jnp.float32)))(*args)
 
 
 def run_outer(*args):
@@ -448,32 +486,43 @@
         pltpu.VMEM((2, LEVELS, 8, COLS), jnp.float32),
         pltpu.VMEM((2, 2, 8, 128), jnp.float32),
     )
-    return call(outer_kernel, f32(32, 16, 128), 11, scratch)(*args)
+    return call(outer_kernel, f32(32, 16, 128), 13, scratch)(*args)
 
 
 def stages(field, row_shift, col_shift, row_frac, col_frac, wave_map, legendre, helm_coef):
     grid_args = (field, row_shift, col_shift, row_frac, col_frac)
-    lat_e, lat_o, lon_e, lon_o = call(edges_kernel, (f32(80, COLS), f32(80, COLS), f32(ROWS, 128), f32(ROWS, 128)), 1)(field)
+    lon_e, lon_o = call(edges_kernel, (f32(ROWS, 128), f32(ROWS, 128)), 1)(field)
     lon_e = lax.ppermute(lon_e, "lon", lon_pairs(0))
     lon_o = lax.ppermute(lon_o, "lon", lon_pairs(1))
-    lat_e, lat_o = call(corner_kernel, (f32(80, COLS), f32(80, COLS)), 4, alias={2: 0, 3: 1})(lon_e, lon_o, lat_e, lat_o)
-    lat_e = lax.ppermute(lat_e, LATF, lat_pairs(0))
-    lat_o = lax.ppermute(lat_o, LATF, lat_pairs(1))
+    edge = (f32(72, COLS), f32(80, COLS), f32(80, COLS))
+    up, down, mirror = call(corner_kernel, edge, 5)(field, lon_e, lon_o, col_shift, col_frac)
+    up = lax.ppermute(up, LATF, lat_shift(1))
+    down = lax.ppermute(down, LATF, lat_shift(-1))
+    mirror = lax.ppermute(mirror, LATF, equator())
+    place = lax.axis_index("y")
+    core = lax.axis_index("core")
+    by_y = legendre.reshape(4, 4, ROWS, DEG)
+    near = lax.dynamic_slice(by_y, (place ^ (1 + core), 0, 0, 0), (1, 4, ROWS, DEG)).reshape(4 * ROWS, DEG)
+    far = lax.dynamic_slice(by_y, (place ^ 3, 2 * core, 0, 0), (1, 2, ROWS, DEG)).reshape(2 * ROWS, DEG)
+    near = lax.ppermute(near, ("y", "core"), [(2 * i + c, 2 * (i ^ (1 + c)) + c) for i in range(4) for c in range(2)])
+    far = lax.ppermute(far, "y", [(i, i ^ 3) for i in range(4)])
+    other = lax.ppermute(jnp.concatenate([near, far], axis=0), "core", [(0, 1), (1, 0)])
     legendre = legendre.reshape(4, 4 * ROWS, DEG)
-    place = lax.axis_index("y")
-    arrived_rows = [
-        lax.ppermute(lax.dynamic_index_in_dim(legendre, place ^ d, 0, keepdims=False), "y", [(i, i ^ d) for i in range(4)])
-        for d in (1, 2, 3)
-    ]
     table = zonal_table(wave_map)
-    inner = run_inner(*grid_args, lon_e, lon_o, table)
-    sent = run_outer(*grid_args, lon_e, lon_o, lat_e, lat_o, table, inner)
+    inner, partial, edge_shift = run_inner(*grid_args, lon_e, lon_o, table)
+    sent = run_outer(field, row_shift, edge_shift, row_frac, col_frac, lon_e, lon_o, up, down, mirror, table, inner, partial)
     arrived = lax.all_to_all(sent, ("y", "lon", "core"), 0, 0, tiled=True)
-    parts = call(legendre_kernel, f32(4, 120, 128), 6, (pltpu.VMEM((4, 32, 256), jnp.float32),), 1)(
-        wave_map, arrived, legendre, *arrived_rows
+    block = f32(120, 128)
+    scratch = (
+        pltpu.VMEM((4, 32, 256), jnp.float32),
+        pltpu.VMEM((4, 120, 128), jnp.float32),
+        pltpu.VMEM((4 * ROWS, DEG), jnp.float32),
+        pltpu.SemaphoreType.DMA(()),
     )
-    parts = lax.all_to_all(parts, "zh", 0, 0, tiled=True)
-    return call(finish_kernel, f32(HALF, 1, 1, 2 * DEG), 2, (), 1)(helm_coef, parts)
+    own, *parts = call(legendre_kernel, (block,) * 4, 6, scratch, 1, whole=2)(wave_map, arrived, legendre, near, far, other)
+    for d in (2, 1, 3):
+        parts[d - 1] = lax.ppermute(parts[d - 1], "zh", [(i, i ^ d) for i in range(4)])
+    return call(finish_kernel, f32(HALF, 1, 1, 2 * DEG), 5, (), 1)(helm_coef, own, *parts)
 
 
 def solution(mesh):

time: 118 us -> 122 us (1.034)
  blocking collectives: 47.6 us -> 16.8 us
  waiting for transfers between devices: 0.02 us -> 22.4 us
  starting transfers between devices: 26.3 us -> 46.2 us
  local copies, waits for them, and re-layouts: 8.54 us -> 3.12 us
  other arithmetic: 3.26 us -> 0.55 us
    all_to_all x1 -> x0, blocking collectives: 23 us -> none  [stages(): parts = lax.all_to_all(parts, 'zh', 0, 0, tiled=True)]
    ppermute x5 -> x9, waiting for transfers between devices: 0.01 us -> 22.4 us  [the longest x3 9.02 us: stages(): lax.ppermute(parts[d - 1], 'zh', [(i, i ^ d) for i in range(4)])]
    ppermute x5 -> x9, starting transfers between devices: 18.7 us -> 39.4 us  [the longest x3 16.2 us: stages(): lax.ppermute(parts[d - 1], 'zh', [(i, i ^ d) for i in range(4)])]
    all_to_all x1, blocking collectives: 24.6 us -> 16.8 us  [stages(): arrived = lax.all_to_all(sent, ('y', 'lon', 'core'), 0, 0, tiled=True)]
    unnamed x16 -> x14, local copies, waits for them, and re-layouts: 3.67 us -> 0.04 us
    squeeze x1 -> x0, local copies, waits for them, and re-layouts: 3.3 us -> none  [stages(): lax.dynamic_index_in_dim(legendre, place ^ d, 0, keepdims=False)]
    dynamic_slice x0 -> x2, local copies, waits for them, and re-layouts: none -> 3.08 us  [the longest x1 1.78 us: stages(): lax.dynamic_slice(by_y, (place ^ 3, 2 * core, 0, 0), (1, 2, ROWS, DEG))]
    div x1, other arithmetic: 2.16 us -> 0.01 us  [zonal_table(): pair = lax.broadcasted_iota(jnp.int32, (64, 128), 1) // 2]
  transfers between devices with their start and end apart: 7 -> 11, of which waited for: 0 -> 4; matrix products, arithmetic and copies ran while one was open for 7% -> 2% of each run, Pallas kernels for 22% -> 23%
where the time goes in v3:
time: 122 us; the launch traced here: 121 us
  starting transfers between devices  46.2 us (38%)
  Pallas kernels  31.9 us (26%)
  waiting for transfers between devices  22.4 us (18%)
  blocking collectives  16.8 us (14%)
  local copies, waits for them, and re-layouts  3.12 us (3%)
    pallas_call x1, Pallas kernels, run_inner(): call(inner_kernel, outs, 8, (shifted(), pltpu.VMEM((LEVELS * 24, COLS), j...  19.3 us
    all_to_all x1, blocking collectives, stages(): arrived = lax.all_to_all(sent, ('y', 'lon', 'core'), 0, 0, tiled=True)  16.8 us
    ppermute x3, starting transfers between devices, stages(): lax.ppermute(parts[d - 1], 'zh', [(i, i ^ d) for i in range(4)])  16.2 us
    ppermute x3, waiting for transfers between devices, stages(): lax.ppermute(parts[d - 1], 'zh', [(i, i ^ d) for i in range(4)])  9.02 us
    ppermute x1, starting transfers between devices, stages(): up = lax.ppermute(up, LATF, lat_shift(1))  8.79 us
    pallas_call x1, Pallas kernels, run_outer(): return call(outer_kernel, f32(32, 16, 128), 13, scratch)(*args)  8.34 us
    ppermute x1, waiting for transfers between devices, stages(): far = lax.ppermute(far, 'y', [(i, i ^ 3) for i in range(4)])  7.62 us
    ppermute x1, waiting for transfers between devices, stages(): down = lax.ppermute(down, LATF, lat_shift(-1))  5.73 us
  transfers between devices with their start and end apart: 11, of which 4 were waited for; matrix products, arithmetic and copies ran while one was open for 2% of the time, Pallas kernels for 23%

profile of v3, /device:TPU:1, one launch (start us, length us, event | category | flops | bytes accessed | tf_op | source)
XLA Modules:
  0.0 121.3 jit_solution(16439658407619057252)
XLA Ops:
  0.0 0.0 copy-start
  0.0 1.3 %constant_dynamic-slice_fusion.1 = f32[1,4,40,1280]{3,2,1,0:T(8,128)S(1)} fusion(f32[4,4,40,1280]{3,2,1,0:T(8,128)} %bitcast.6, s32[]{:T(128)S(6)} %select_n.61), kind=kLoop, calls=%fused_computation.28 | loop fusion | bytes 1638404 | tf_op jit(solution)/shard_map/dynamic_slice | solution.py:505
  1.3 5.6 %collective-permute-start.5 = (f32[160,1280]{1,0:T(8,128)S(1)}, f32[160,1280]{1,0:T(8,128)S(1)}, u32[]{:S(2)}, u32[]{:S(2)}) collective-permute-start(f32[160,1280]{1,0:T(8,128)S(1)} %bitcast.9), channel_id=1, source_target_pairs={{0,128},{1,257},{128,0},{129,385},{256,384},{257,1},{384,256},{385... | collective-permute-start | bytes 2457608 | tf_op jit(solution)/shard_map/ppermute | solution.py:507
  7.0 1.8 %constant_dynamic-slice_fusion = f32[1,2,40,1280]{3,2,1,0:T(8,128)} fusion(f32[4,4,40,1280]{3,2,1,0:T(8,128)} %bitcast.7, s32[]{:T(128)S(6)} %select_n.62, s32[]{:T(128)S(6)} %select_n.63), kind=kLoop, calls=%fused_computation.27 | loop fusion | bytes 819208 | tf_op jit(solution)/shard_map/dynamic_slice | solution.py:506
  8.7 2.7 %collective-permute-start.6 = (f32[80,1280]{1,0:T(8,128)}, f32[80,1280]{1,0:T(8,128)S(1)}, u32[]{:S(2)}, u32[]{:S(2)}) collective-permute-start(f32[80,1280]{1,0:T(8,128)} %bitcast.4), channel_id=1, source_target_pairs={{0,384},{128,256},{256,128},{384,0},{1,385},{129,257},{257,129},{3... | collective-permute-start | bytes 1228808 | tf_op jit(solution)/shard_map/ppermute | solution.py:508
  11.4 0.0 copy-done
  11.4 0.2 shard_map.82
  11.6 3.1 %collective-permute-start = (f32[40,128]{1,0:T(8,128)S(1)}, f32[40,128]{1,0:T(8,128)S(1)}, u32[]{:S(2)}, u32[]{:S(2)}) collective-permute-start(f32[40,128]{1,0:T(8,128)S(1)} %get-tuple-element.17), channel_id=1, source_target_pairs={{0,8},{8,0},{16,24},{24,16},{1,9},{9,1},{17,25},{25,17},{2,10},{10... | collective-permute-start | bytes 61448 | tf_op jit(solution)/shard_map/ppermute | solution.py:495
  14.8 3.7 %collective-permute-start.1 = (f32[40,128]{1,0:T(8,128)S(1)}, f32[40,128]{1,0:T(8,128)S(1)}, u32[]{:S(2)}, u32[]{:S(2)}) collective-permute-start(f32[40,128]{1,0:T(8,128)S(1)} %get-tuple-element.18), channel_id=1, source_target_pairs={{8,16},{16,8},{24,0},{0,24},{9,17},{17,9},{25,1},{1,25},{10,18},{1... | collective-permute-start | bytes 61448 | tf_op jit(solution)/shard_map/ppermute | solution.py:496
  18.5 0.0 copy-start.5
  18.5 0.0 copy-start.1
  18.5 0.0 copy-start.3
  18.5 7.6 %collective-permute-done.6.far = f32[80,1280]{1,0:T(8,128)S(1)} collective-permute-done((f32[80,1280]{1,0:T(8,128)}, f32[80,1280]{1,0:T(8,128)S(1)}, u32[]{:S(2)}, u32[]{:S(2)}) %collective-permute-start.6) | collective-permute-done | bytes 409632 | tf_op jit(solution)/shard_map/ppermute | solution.py:508
  26.2 0.0 collective-permute-done.5.near
  26.2 0.1 pad_maximum_fusion
  26.3 4.1 %collective-permute-start.7 = (f32[240,1280]{1,0:T(8,128)S(1)}, f32[240,1280]{1,0:T(8,128)S(1)}, u32[]{:S(2)}, u32[]{:S(2)}) collective-permute-start(f32[240,1280]{1,0:T(8,128)S(1)} %pad_maximum_fusion), channel_id=1, source_target_pairs={{0,1},{1,0},{2,3},{3,2},{4,5},{5,4},{6,7},{7,6},{8,9},{9,8},{10,11... | collective-permute-start | bytes 3686408 | tf_op jit(solution)/shard_map/ppermute | solution.py:509
  30.4 0.0 copy-done.5
  30.4 0.1 select_reduce_fusion
  30.5 0.3 cosine_multiply_fusion
  30.8 0.1 fusion.10
  30.8 0.0 copy-start.2
  30.8 0.0 copy-start.4
  30.8 0.0 collective-permute-done.lon_even
  30.8 0.0 collective-permute-done.1.lon_odd
  30.9 0.0 copy-done.1
  30.9 0.0 copy-done.3
  30.9 0.1 shard_map.84
  31.0 8.8 %collective-permute-start.2 = (f32[72,640]{1,0:T(8,128)S(1)}, f32[72,640]{1,0:T(8,128)S(1)}, u32[]{:S(2)}, u32[]{:S(2)}) collective-permute-start(f32[72,640]{1,0:T(8,128)S(1)} %get-tuple-element.20), channel_id=1, source_target_pairs={{0,32},{1,33},{2,34},{3,35},{4,36},{5,37},{6,38},{7,39},{32,64},{3... | collective-permute-start | bytes 552968 | tf_op jit(solution)/shard_map/ppermute | solution.py:499
  39.8 1.3 %collective-permute-start.3 = (f32[80,640]{1,0:T(8,128)S(1)}, f32[80,640]{1,0:T(8,128)S(1)}, u32[]{:S(2)}, u32[]{:S(2)}) collective-permute-start(f32[80,640]{1,0:T(8,128)S(1)} %get-tuple-element.21), channel_id=1, source_target_pairs={{32,0},{33,1},{34,2},{35,3},{36,4},{37,5},{38,6},{39,7},{64,32},{6... | collective-permute-start | bytes 614408 | tf_op jit(solution)/shard_map/ppermute | solution.py:500
  41.1 0.7 collective-permute-start.4
  41.9 0.0 copy-done.2
  41.9 0.0 copy-done.4
  41.9 19.3 %shard_map.83 = (f32[288,128]{1,0:T(8,128)S(1)}, f32[192,640]{1,0:T(8,128)S(1)}, s32[192,640]{1,0:T(8,128)S(1)}) custom-call(f32[1,12,40,640]{3,2,1,0:T(8,128)S(1)} %copy-done, s32[1,12,40,640]{3,2,1,0:T(8,128)S(1)} %copy-done.2, s32[1,12,40,640]{3,2,1,0:T(8,128)} %_shift.1, bf16[1,12,40,640]{3,2,1,0:T(8,128)(2,1)S(1)} %copy-done.4, ...), custom_call_target="tpu_custom_call" | custom-call | tf_op jit(solution)/shard_map/pallas_call | solution.py:478
  61.1 0.0 collective-permute-done.2.up
  61.2 5.7 %collective-permute-done.3.down = f32[80,640]{1,0:T(8,128)S(1)} collective-permute-done((f32[80,640]{1,0:T(8,128)S(1)}, f32[80,640]{1,0:T(8,128)S(1)}, u32[]{:S(2)}, u32[]{:S(2)}) %collective-permute-start.3) | collective-permute-done | bytes 204832 | tf_op jit(solution)/shard_map/ppermute | solution.py:500
  66.9 0.0 collective-permute-done.4.mirror
  66.9 8.3 %shard_map.85 = f32[32,16,128]{2,1,0:T(8,128)S(1)} custom-call(f32[1,12,40,640]{3,2,1,0:T(8,128)S(1)} %copy-done, s32[1,12,40,640]{3,2,1,0:T(8,128)S(1)} %copy-done.2, s32[192,640]{1,0:T(8,128)S(1)} %get-tuple-element.19.col_shift, bf16[1,12,40,640]{3,2,1,0:T(8,128)(2,1)S(1)} %copy-done.4, bf16[1,12,40,640]{3,2,1,0:T(8,128)(2,1)S(1)} %copy-done.1, ...), custom_call_target="tpu_custom_call" | custom-call | tf_op jit(solution)/shard_map/pallas_call | solution.py:489
  75.2 16.8 %all_to_all.5.arrived = f32[32,16,128]{2,1,0:T(8,128)S(1)} all-to-all(f32[32,16,128]{2,1,0:T(8,128)S(1)} %shard_map.85), channel_id=1, replica_groups=mesh['y'=4,'zh'=4,'lon'=4,'zl'=4,'core'=2] {'y','lon','core'}, dimensions={0} | all-to-all | bytes 524288 | tf_op jit(solution)/shard_map/all_to_all | solution.py:514
  92.1 0.0 collective-permute-done.7.other
  92.1 2.7 %shard_map.86 = (f32[120,128]{1,0:T(8,128)S(1)}, f32[120,128]{1,0:T(8,128)S(1)}, f32[120,128]{1,0:T(8,128)S(1)}, f32[120,128]{1,0:T(8,128)S(1)}) custom-call(s32[64]{0:T(128)S(1)} %copy-done.5, f32[32,16,128]{2,1,0:T(8,128)S(1)} %all_to_all.5.arrived, f32[4,160,1280]{2,1,0:T(8,128)} %bitcast.8, f32[160,1280]{1,0:T(8,128)S(1)} %collective-permute-done.5.near, ...), custom_call_target="tpu_custom_call" | custom-call | tf_op jit(solution)/shard_map/pallas_call | solution.py:522
  94.8 7.1 %collective-permute-start.8 = (f32[120,128]{1,0:T(8,128)S(1)}, f32[120,128]{1,0:T(8,128)S(1)}, u32[]{:S(2)}, u32[]{:S(2)}) collective-permute-start(f32[120,128]{1,0:T(8,128)S(1)} %get-tuple-element.26), channel_id=1, source_target_pairs={{0,32},{32,0},{64,96},{96,64},{1,33},{33,1},{65,97},{97,65},{2,34}... | collective-permute-start | bytes 184328 | tf_op jit(solution)/shard_map/ppermute | solution.py:524
  101.9 6.6 %collective-permute-start.9 = (f32[120,128]{1,0:T(8,128)S(1)}, f32[120,128]{1,0:T(8,128)S(1)}, u32[]{:S(2)}, u32[]{:S(2)}) collective-permute-start(f32[120,128]{1,0:T(8,128)S(1)} %get-tuple-element.27), channel_id=1, source_target_pairs={{0,64},{32,96},{64,0},{96,32},{1,65},{33,97},{65,1},{97,33},{2,66}... | collective-permute-start | bytes 184328 | tf_op jit(solution)/shard_map/ppermute | solution.py:524
  108.6 2.4 %collective-permute-start.10 = (f32[120,128]{1,0:T(8,128)S(1)}, f32[120,128]{1,0:T(8,128)S(1)}, u32[]{:S(2)}, u32[]{:S(2)}) collective-permute-start(f32[120,128]{1,0:T(8,128)S(1)} %get-tuple-element.28), channel_id=1, source_target_pairs={{0,96},{32,64},{64,32},{96,0},{1,97},{33,65},{65,33},{97,1},{2,98}... | collective-permute-start | bytes 184328 | tf_op jit(solution)/shard_map/ppermute | solution.py:524
  111.0 0.0 collective-permute-done.8.part_1
  111.0 6.5 %collective-permute-done.9.part_2 = f32[120,128]{1,0:T(8,128)S(1)} collective-permute-done((f32[120,128]{1,0:T(8,128)S(1)}, f32[120,128]{1,0:T(8,128)S(1)}, u32[]{:S(2)}, u32[]{:S(2)}) %collective-permute-start.9) | collective-permute-done | bytes 61472 | tf_op jit(solution)/shard_map/ppermute | solution.py:524
  117.5 2.5 %collective-permute-done.10.part_3 = f32[120,128]{1,0:T(8,128)S(1)} collective-permute-done((f32[120,128]{1,0:T(8,128)S(1)}, f32[120,128]{1,0:T(8,128)S(1)}, u32[]{:S(2)}, u32[]{:S(2)}) %collective-permute-start.10) | collective-permute-done | bytes 61472 | tf_op jit(solution)/shard_map/ppermute | solution.py:524
  120.0 0.0 copy-done.6
  120.0 1.2 %shard_map.87 = f32[6,1,1,2560]{3,2,1,0:T(1,128)} custom-call(f32[6]{0:T(128)S(1)} %copy-done.6, f32[120,128]{1,0:T(8,128)S(1)} %get-tuple-element.25.own, f32[120,128]{1,0:T(8,128)S(1)} %collective-permute-done.8.part_1, f32[120,128]{1,0:T(8,128)S(1)} %collective-permute-done.9.part_2, f32[120,128]{1,0:T(8,128)S(1)} %collective-permute-done.10.part_3), custom_call_target="tpu_custom_call" | custom-call | tf_op jit(solution)/shard_map/pallas_call | solution.py:525
  (6 shorter events, 0.1 us)
Async XLA Ops:
  0.0 11.4 %copy-start = (f32[1,12,40,640]{3,2,1,0:T(8,128)S(1)}, f32[1,12,40,640]{3,2,1,0:T(8,128)}, u32[]{:S(2)}) copy-start(f32[1,12,40,640]{3,2,1,0:T(8,128)} %field.7) | copy-start | bytes 3686404
  1.3 24.9 %collective-permute-start.5 = (f32[160,1280]{1,0:T(8,128)S(1)}, f32[160,1280]{1,0:T(8,128)S(1)}, u32[]{:S(2)}, u32[]{:S(2)}) collective-permute-start(f32[160,1280]{1,0:T(8,128)S(1)} %bitcast.9), channel_id=1, source_target_pairs={{0,128},{1,257},{128,0},{129,385},{256,384},{257,1},{384,256},{385... | collective-permute-start | bytes 2457608 | tf_op jit(solution)/shard_map/ppermute | solution.py:507
  8.7 17.4 %collective-permute-start.6 = (f32[80,1280]{1,0:T(8,128)}, f32[80,1280]{1,0:T(8,128)S(1)}, u32[]{:S(2)}, u32[]{:S(2)}) collective-permute-start(f32[80,1280]{1,0:T(8,128)} %bitcast.4), channel_id=1, source_target_pairs={{0,384},{128,256},{256,128},{384,0},{1,385},{129,257},{257,129},{3... | collective-permute-start | bytes 1228808 | tf_op jit(solution)/shard_map/ppermute | solution.py:508
  11.6 19.2 %collective-permute-start = (f32[40,128]{1,0:T(8,128)S(1)}, f32[40,128]{1,0:T(8,128)S(1)}, u32[]{:S(2)}, u32[]{:S(2)}) collective-permute-start(f32[40,128]{1,0:T(8,128)S(1)} %get-tuple-element.17), channel_id=1, source_target_pairs={{0,8},{8,0},{16,24},{24,16},{1,9},{9,1},{17,25},{25,17},{2,10},{10... | collective-permute-start | bytes 61448 | tf_op jit(solution)/shard_map/ppermute | solution.py:495
  14.8 16.1 %collective-permute-start.1 = (f32[40,128]{1,0:T(8,128)S(1)}, f32[40,128]{1,0:T(8,128)S(1)}, u32[]{:S(2)}, u32[]{:S(2)}) collective-permute-start(f32[40,128]{1,0:T(8,128)S(1)} %get-tuple-element.18), channel_id=1, source_target_pairs={{8,16},{16,8},{24,0},{0,24},{9,17},{17,9},{25,1},{1,25},{10,18},{1... | collective-permute-start | bytes 61448 | tf_op jit(solution)/shard_map/ppermute | solution.py:496
  18.5 11.9 %copy-start.5 = (s32[64]{0:T(128)S(1)}, s32[64]{0:T(128)}, u32[]{:S(2)}) copy-start(s32[64]{0:T(128)} %wave_map.1) | copy-start | bytes 772
  18.5 12.3 %copy-start.1 = (bf16[1,12,40,640]{3,2,1,0:T(8,128)(2,1)S(1)}, bf16[1,12,40,640]{3,2,1,0:T(8,128)(2,1)}, u32[]{:S(2)}) copy-start(bf16[1,12,40,640]{3,2,1,0:T(8,128)(2,1)} %col_frac.3) | copy-start | bytes 1843204
  18.5 12.3 %copy-start.3 = (s32[1,12,40,640]{3,2,1,0:T(8,128)S(1)}, s32[1,12,40,640]{3,2,1,0:T(8,128)}, u32[]{:S(2)}) copy-start(s32[1,12,40,640]{3,2,1,0:T(8,128)} %_shift.1) | copy-start | bytes 3686404
  26.3 65.8 %collective-permute-start.7 = (f32[240,1280]{1,0:T(8,128)S(1)}, f32[240,1280]{1,0:T(8,128)S(1)}, u32[]{:S(2)}, u32[]{:S(2)}) collective-permute-start(f32[240,1280]{1,0:T(8,128)S(1)} %pad_maximum_fusion), channel_id=1, source_target_pairs={{0,1},{1,0},{2,3},{3,2},{4,5},{5,4},{6,7},{7,6},{8,9},{9,8},{10,11... | collective-permute-start | bytes 3686408 | tf_op jit(solution)/shard_map/ppermute | solution.py:509
  30.8 11.1 %copy-start.2 = (s32[1,12,40,640]{3,2,1,0:T(8,128)S(1)}, s32[1,12,40,640]{3,2,1,0:T(8,128)}, u32[]{:S(2)}) copy-start(s32[1,12,40,640]{3,2,1,0:T(8,128)} %row_shift.3) | copy-start | bytes 3686404
  30.8 11.1 %copy-start.4 = (bf16[1,12,40,640]{3,2,1,0:T(8,128)(2,1)S(1)}, bf16[1,12,40,640]{3,2,1,0:T(8,128)(2,1)}, u32[]{:S(2)}) copy-start(bf16[1,12,40,640]{3,2,1,0:T(8,128)(2,1)} %row_frac.3) | copy-start | bytes 1843204
  31.0 30.1 %collective-permute-start.2 = (f32[72,640]{1,0:T(8,128)S(1)}, f32[72,640]{1,0:T(8,128)S(1)}, u32[]{:S(2)}, u32[]{:S(2)}) collective-permute-start(f32[72,640]{1,0:T(8,128)S(1)} %get-tuple-element.20), channel_id=1, source_target_pairs={{0,32},{1,33},{2,34},{3,35},{4,36},{5,37},{6,38},{7,39},{32,64},{3... | collective-permute-start | bytes 552968 | tf_op jit(solution)/shard_map/ppermute | solution.py:499
  39.8 27.1 %collective-permute-start.3 = (f32[80,640]{1,0:T(8,128)S(1)}, f32[80,640]{1,0:T(8,128)S(1)}, u32[]{:S(2)}, u32[]{:S(2)}) collective-permute-start(f32[80,640]{1,0:T(8,128)S(1)} %get-tuple-element.21), channel_id=1, source_target_pairs={{32,0},{33,1},{34,2},{35,3},{36,4},{37,5},{38,6},{39,7},{64,32},{6... | collective-permute-start | bytes 614408 | tf_op jit(solution)/shard_map/ppermute | solution.py:500
  41.1 25.8 %collective-permute-start.4 = (f32[80,640]{1,0:T(8,128)S(1)}, f32[80,640]{1,0:T(8,128)S(1)}, u32[]{:S(2)}, u32[]{:S(2)}) collective-permute-start(f32[80,640]{1,0:T(8,128)S(1)} %get-tuple-element.22), channel_id=1, source_target_pairs={{480,481},{481,480},{482,483},{483,482},{484,485},{485,484},{486,4... | collective-permute-start | bytes 614408 | tf_op jit(solution)/shard_map/ppermute | solution.py:501
  92.1 27.9 %copy-start.6 = (f32[6]{0:T(128)S(1)}, f32[6]{0:T(128)}, u32[]{:S(2)}) copy-start(f32[6]{0:T(128)} %helm.1) | copy-start | bytes 76
  94.8 16.2 %collective-permute-start.8 = (f32[120,128]{1,0:T(8,128)S(1)}, f32[120,128]{1,0:T(8,128)S(1)}, u32[]{:S(2)}, u32[]{:S(2)}) collective-permute-start(f32[120,128]{1,0:T(8,128)S(1)} %get-tuple-element.26), channel_id=1, source_target_pairs={{0,32},{32,0},{64,96},{96,64},{1,33},{33,1},{65,97},{97,65},{2,34}... | collective-permute-start | bytes 184328 | tf_op jit(solution)/shard_map/ppermute | solution.py:524
  101.9 15.6 %collective-permute-start.9 = (f32[120,128]{1,0:T(8,128)S(1)}, f32[120,128]{1,0:T(8,128)S(1)}, u32[]{:S(2)}, u32[]{:S(2)}) collective-permute-start(f32[120,128]{1,0:T(8,128)S(1)} %get-tuple-element.27), channel_id=1, source_target_pairs={{0,64},{32,96},{64,0},{96,32},{1,65},{33,97},{65,1},{97,33},{2,66}... | collective-permute-start | bytes 184328 | tf_op jit(solution)/shard_map/ppermute | solution.py:524
  108.6 11.5 %collective-permute-start.10 = (f32[120,128]{1,0:T(8,128)S(1)}, f32[120,128]{1,0:T(8,128)S(1)}, u32[]{:S(2)}, u32[]{:S(2)}) collective-permute-start(f32[120,128]{1,0:T(8,128)S(1)} %get-tuple-element.28), channel_id=1, source_target_pairs={{0,96},{32,64},{64,32},{96,0},{1,97},{33,65},{65,33},{97,1},{2,98}... | collective-permute-start | bytes 184328 | tf_op jit(solution)/shard_map/ppermute | solution.py:524
